TPU v7x, 32 devices: a whole 2x2x4 slice. The times are simulated.
32 devices in a mesh: pop: 8 (over z, y), merge: 4 (over x, core).
Axes of the slice: x: 2, y: 2, z: 4, core: 2. Of those that a mesh axis runs over, the one named last changes fastest.
Arguments:
- slab: float32 [256, 256, 4096], P('pop', 'merge'), may hold values from -6 to 6
- sample_counts: int32 [2], replicated, may hold values from 160 to 255
- mode_rows_one: float32 [96, 256], replicated, may hold values from -0.375 to 0.375
- mode_rows_two: float32 [96, 256], replicated, may hold values from -0.375 to 0.375
- merge_tensor: float32 [96, 96, 96], replicated, may hold values from -0.0625 to 0.0625
- ancestral_modes: float32 [96, 256], replicated, may hold values from -0.625 to 0.625
Outputs:
- merged: float32 [4096, 256], P(('pop', 'merge'))
All inputs are finite; a program needn't handle non-finite values.
Results may differ from a plain program's by a relative error of at most 0.000076.
Values sent between devices are 32-bit elements; how exact they have to be, the bound alone decides.
No kernel may reach another device: no remote copies, remote signals or barrier semaphores. Data moves between devices by JAX's collectives and lax.ppermute only.
A program may use at most 128 MiB of HBM per device.

v0:
```python
import jax
import jax.numpy as jnp
from jax import lax
from jax.sharding import PartitionSpec as P

branch_one = 0.00025
branch_two = 0.0004


def prepared(rows, count, branch):
    order = jnp.arange(rows.shape[0], dtype=jnp.float32)
    decay = jnp.exp(-branch * order * (order + 1.0) / 2.0)
    keep = jnp.arange(rows.shape[1], dtype=jnp.int32) <= count
    return jnp.where(keep[None, :], rows, jnp.zeros_like(rows)) * decay[:, None]


def on_device(slab, sample_counts, mode_rows_one, mode_rows_two, merge_tensor, ancestral_modes):
    high = lax.Precision.HIGHEST
    modes = mode_rows_one.shape[0]
    proj_one = prepared(mode_rows_one, sample_counts[0], branch_one)
    proj_two = prepared(mode_rows_two, sample_counts[1], branch_two)
    rows_one = slab.shape[0]
    rows_two = slab.shape[1]
    begin_one = lax.axis_index("pop") * rows_one
    begin_two = lax.axis_index("merge") * rows_two
    local_one = lax.dynamic_slice_in_dim(proj_one, begin_one, rows_one, 1)
    local_two = lax.dynamic_slice_in_dim(proj_two, begin_two, rows_two, 1)
    folded_local = jnp.einsum("mnj,nb->jmb", merge_tensor, local_two, precision=high)
    weave = jnp.einsum("ma,jmb->abj", local_one, folded_local, precision=high).reshape(
        rows_one * rows_two, modes
    )
    flat_slab = slab.reshape(rows_one * rows_two, -1)
    summed = lax.psum_scatter(
        lax.dot_general(flat_slab, weave, (((0,), (0,)), ((), ())), precision=high),
        ("pop", "merge"),
        scatter_dimension=0,
        tiled=True,
    )
    return jnp.dot(summed, ancestral_modes, precision=high)


def solution(mesh):
    in_specs = (P("pop", "merge", None), P(), P(), P(), P(), P())
    out_specs = P(("pop", "merge"), None)
    return jax.shard_map(
        on_device, mesh=mesh, in_specs=in_specs, out_specs=out_specs, check_vma=False
    )
```

profile of v0, /device:TPU:0, one launch (start us, length us, event | category | flops | bytes accessed | tf_op | source)
XLA Modules:
  0.0 174.9 jit_solution(13488684722700495997)
XLA Ops:
  6.5 0.0 copy-start
  6.5 0.0 copy-start.1
  6.5 0.0 reduce-scatter.2.cloned.1.call-start
  6.6 1.4 fusion.34
  7.9 0.6 iota_compare_fusion
  8.6 0.6 iota_compare_fusion.1
  9.2 0.1 dynamic-slice.1
  9.3 0.1 dynamic-slice
  9.4 4.9 %fusion.16 = f32[64,96,96]{2,0,1:T(8,128)S(1)} fusion(f32[96,96,96]{2,1,0:T(8,128)} %param.10, f32[96,256]{1,0:T(8,128)} %param.9, s32[]{:T(128)S(6)} %select_n.14, f32[96]{0:T(128)S(1)} %fusion.27, pred[64]{0:T(512)(128)(4,1)S(1)} %dynamic-slice), kind=kOutput, calls=%fused_computation.13 | convolution fusion | flops 679489536 | bytes 7127492 | tf_op jit(solution)/shard_map/mnj,nb->jmb/dot_general | solution.py:28
  14.2 0.0 copy-done.1
  14.2 3.7 %fusion.8 = f32[32,64,96]{2,0,1:T(8,128)S(1)} fusion(f32[64,96,96]{2,0,1:T(8,128)S(1)} %fusion.16, f32[96,256]{1,0:T(8,128)S(1)} %copy-done.1, s32[]{:T(128)S(6)} %select_n.16, f32[96]{0:T(128)S(1)} %fusion.29, pred[32]{0:T(512)(128)(4,1)S(1)} %dynamic-slice.1), kind=kOutput, calls=%fused_computation.6 | convolution fusion | flops 226498560 | bytes 3982340 | tf_op jit(solution)/shard_map/ma,jmb->abj/dot_general | solution.py:29
  17.9 47.7 %fusion.2 = f32[4096,96]{0,1:T(8,128)} fusion(f32[32,64,96]{2,0,1:T(8,128)S(1)} %fusion.8, f32[32,64,4096]{2,1,0:T(8,128)} %param.6), kind=kOutput, calls=%fused_computation.2 | convolution fusion | flops 9663676416 | bytes 35913728 | tf_op jit(solution)/shard_map/dot_general | solution.py:34
  65.6 0.0 reduce-scatter.2.cloned.1.call-update
  65.6 100.7 %reduce-scatter.2.cloned.1.call-done = f32[128,96]{0,1:T(8,128)} async-done(((f32[4096,96]{0,1:T(8,128)}), f32[128,96]{0,1:T(8,128)}) %reduce-scatter.2.cloned.1.call-update) | async-done | bytes 49168 | tf_op jit(solution)/shard_map/reduce_scatter | solution.py:33
  166.3 0.0 copy-done
  166.3 1.8 %fusion.35 = f32[128,256]{1,0:T(8,128)} fusion(f32[128,96]{0,1:T(8,128)} %reduce-scatter.2.cloned.1.call-done, f32[96,256]{1,0:T(8,128)S(1)} %copy-done), kind=kOutput, calls=%fused_computation.35 | convolution fusion | flops 37748736 | bytes 278528 | tf_op jit(solution)/shard_map/dot_general | solution.py:39
  (2 shorter events, 0.0 us)
Async XLA Ops:
  6.5 159.8 %copy-start = (f32[96,256]{1,0:T(8,128)S(1)}, f32[96,256]{1,0:T(8,128)}, u32[]{:S(2)}) copy-start(f32[96,256]{1,0:T(8,128)} %param.11) | copy-start | bytes 294916
  6.5 7.7 %copy-start.1 = (f32[96,256]{1,0:T(8,128)S(1)}, f32[96,256]{1,0:T(8,128)}, u32[]{:S(2)}) copy-start(f32[96,256]{1,0:T(8,128)} %param.8) | copy-start | bytes 294916
  6.5 159.8 %reduce-scatter.2.cloned.1.call-start = ((), (), s32[]{:S(2)}) async-start(), calls=%async_computation.1 | async-start | bytes 1622016 | tf_op jit(solution)/shard_map/reduce_scatter | solution.py:33
Sparse Core Ops, SparseCore 0:
  65.8 100.5 reduce-scatter.1
where the time goes:
time: 175 us
  waiting for transfers between devices  101 us (58%)
  matrix products  58 us (33%)
  between operations  13.4 us (8%)
    reduce_scatter x1, waiting for transfers between devices, on_device(): lax.psum_scatter(lax.dot_general(flat_slab, weave, (((0,), (0,)), ((), ()...  101 us
    dot_general x1, matrix products, on_device(): lax.dot_general(flat_slab, weave, (((0,), (0,)), ((), ())), precision=high)  47.7 us
    dot_general x1, matrix products, on_device(): jnp.einsum('mnj,nb->jmb', merge_tensor, local_two, precision=high)  4.86 us
    dot_general x1, matrix products, on_device(): jnp.einsum('ma,jmb->abj', local_one, folded_local, precision=high)  3.67 us
  transfers between devices with their start and end apart: 1, of which 1 were waited for; matrix products, arithmetic and copies ran while one was open for 0% of the time, Pallas kernels for 0%

commit v1 on v0

v1 whole, which is shorter than its diff:
```python
import jax
import jax.numpy as jnp
from jax import lax
from jax.experimental import pallas as pl
from jax.experimental.pallas import tpu as pltpu
from jax.sharding import PartitionSpec as P

branch_one = 0.00025
branch_two = 0.0004
AXES = ("pop", "merge")
LANES = 128


def prepared(rows, count, branch):
    order = jnp.arange(rows.shape[0], dtype=jnp.float32)
    decay = jnp.exp(-branch * order * (order + 1.0) / 2.0)
    keep = jnp.arange(rows.shape[1], dtype=jnp.int32) <= count
    return jnp.where(keep[None, :], rows, jnp.zeros_like(rows)) * decay[:, None]


def split(value):
    high = lax.reduce_precision(value, 8, 7)
    return high.astype(jnp.bfloat16), (value - high).astype(jnp.bfloat16)


def split_block(value):
    high = value.astype(jnp.bfloat16)
    return high, (value - high.astype(jnp.float32)).astype(jnp.bfloat16)


def partial_sums(slab, weave, pops, merges, wide):
    rows, cols = slab.shape
    modes = weave.shape[0] // 2
    per = cols // (pops * merges)

    def body(where, slab_ref, weave_ref, out_ref):
        high, low = split_block(slab_ref[...])
        two = jnp.dot(weave_ref[...], high, preferred_element_type=jnp.float32)
        one = jnp.dot(weave_ref[:modes], low, preferred_element_type=jnp.float32)
        value = two[:modes] + (two[modes:] + one)
        for m in range(merges):
            out_ref[0, jnp.bitwise_xor(where[1], m)] = value[:, m * per : (m + 1) * per]

    return pl.pallas_call(
        body,
        out_shape=jax.ShapeDtypeStruct((pops, merges, modes, per), jnp.float32),
        grid_spec=pltpu.PrefetchScalarGridSpec(
            num_scalar_prefetch=1,
            grid=(pops,),
            in_specs=[
                pl.BlockSpec((rows, merges * per), lambda i, where: (0, jnp.bitwise_xor(i, where[0]))),
                pl.BlockSpec(weave.shape, lambda i, where: (0, 0)),
            ],
            out_specs=pl.BlockSpec((1, merges, modes, per), lambda i, where: (i, 0, 0, 0)),
        ),
        compiler_params=pltpu.CompilerParams(vmem_limit_bytes=48 * 1024 * 1024),
    )(jnp.stack([lax.axis_index("pop"), lax.axis_index("merge")]).astype(jnp.int32), slab, weave)


def scatter_sum(value, devices):
    bits = [1 << k for k in reversed(range(devices.bit_length() - 1))]
    value = value.reshape((2,) * len(bits) + value.shape[-2:])
    for group in ([bits[-1]], bits[1:-1], [bits[0]]):
        combos = [0]
        for bit in group:
            combos = combos + [c | bit for c in combos]

        def piece(c):
            return value[tuple((1 if c & b else 0) if b in group else slice(None) for b in bits)]

        sent = [
            lax.ppermute(piece(c), AXES, [(i, i ^ c) for i in range(devices)]) for c in combos[1:]
        ]
        total = piece(0)
        for part in sent:
            total = total + part
        value = total
        bits = [b for b in bits if b not in group]
    return value


def on_device(pops, merges):
    devices = pops * merges

    def run(slab, sample_counts, mode_rows_one, mode_rows_two, merge_tensor, ancestral_modes):
        high = lax.Precision.HIGHEST
        modes = mode_rows_one.shape[0]
        proj_one = prepared(mode_rows_one, sample_counts[0], branch_one)
        proj_two = prepared(mode_rows_two, sample_counts[1], branch_two)
        rows_one, rows_two, cols = slab.shape
        begin_one = lax.axis_index("pop") * rows_one
        begin_two = lax.axis_index("merge") * rows_two
        local_one = lax.dynamic_slice_in_dim(proj_one, begin_one, rows_one, 1)
        local_two = lax.dynamic_slice_in_dim(proj_two, begin_two, rows_two, 1)
        folded_local = jnp.einsum("mnj,nb->jmb", merge_tensor, local_two, precision=high)
        weave = jnp.einsum("ma,jmb->jab", local_one, folded_local, precision=high)
        weave = weave.reshape(modes, rows_one * rows_two)
        flat_slab = slab.reshape(rows_one * rows_two, cols)
        two_power = devices & (devices - 1) == 0 and pops > 2 and merges > 1
        if two_power and cols % (devices * LANES) == 0:
            parts = partial_sums(flat_slab, jnp.concatenate(split(weave)), pops, merges, 0)
            summed = scatter_sum(parts, devices)
        else:
            summed = lax.psum_scatter(
                lax.dot_general(weave, flat_slab, (((1,), (0,)), ((), ())), precision=high),
                AXES,
                scatter_dimension=1,
                tiled=True,
            )
        return lax.dot_general(summed, ancestral_modes, (((0,), (0,)), ((), ())), precision=high)

    return run


def solution(mesh):
    in_specs = (P("pop", "merge", None), P(), P(), P(), P(), P())
    out_specs = P(AXES, None)
    run = on_device(mesh.shape["pop"], mesh.shape["merge"])
    return jax.shard_map(run, mesh=mesh, in_specs=in_specs, out_specs=out_specs, check_vma=False)
```

time: 175 us -> 63.5 us (0.36)
  waiting for transfers between devices: 101 us -> 9.23 us
  matrix products: 58 us -> 14.8 us
  Pallas kernels: 0 us -> 15.5 us
  starting transfers between devices: 0.01 us -> 15.1 us
  between operations: 13.4 us -> 0.12 us
  local copies, waits for them, and re-layouts: 1.52 us -> 6.74 us
    reduce_scatter x1 -> x0, waiting for transfers between devices: 101 us -> none  [on_device(): lax.psum_scatter(lax.dot_general(flat_slab, weave, (((0,), (0,)), ((), ()...]
    dot_general x4 -> x3, matrix products: 58 us -> 14.8 us  [the longest x1 7.26 us: run(): jnp.einsum('mnj,nb->jmb', merge_tensor, local_two, precision=high)]
    pallas_call x0 -> x1, Pallas kernels: none -> 15.5 us  [partial_sums(): pl.pallas_call(body, out_shape=jax.ShapeDtypeStruct((pops, merges, modes,...]
    ppermute x0 -> x9, starting transfers between devices: none -> 15.1 us  [scatter_sum(): lax.ppermute(piece(c), AXES, [(i, i ^ c) for i in range(devices)])]
    ppermute x0 -> x9, waiting for transfers between devices: none -> 9.23 us  [scatter_sum(): lax.ppermute(piece(c), AXES, [(i, i ^ c) for i in range(devices)])]
    dot_general x0 -> x1, local copies, waits for them, and re-layouts: none -> 3.12 us  [run(): jnp.einsum('mnj,nb->jmb', merge_tensor, local_two, precision=high)]
  transfers between devices with their start and end apart: 1 -> 9, of which waited for: 1 -> 5; matrix products, arithmetic and copies ran while one was open for 0% -> 0% of each run, Pallas kernels for 0% -> 0%
where the time goes in v1:
time: 63.5 us; the launch traced here: 63.1 us
  Pallas kernels  15.5 us (24%)
  starting transfers between devices  15.1 us (24%)
  matrix products  14.8 us (23%)
  waiting for transfers between devices  9.23 us (15%)
  local copies, waits for them, and re-layouts  6.74 us (11%)
  other arithmetic  1.62 us (3%)
    pallas_call x1, Pallas kernels, partial_sums(): pl.pallas_call(body, out_shape=jax.ShapeDtypeStruct((pops, merges, modes,...  15.5 us
    ppermute x9, starting transfers between devices, scatter_sum(): lax.ppermute(piece(c), AXES, [(i, i ^ c) for i in range(devices)])  15.1 us
    ppermute x9, waiting for transfers between devices, scatter_sum(): lax.ppermute(piece(c), AXES, [(i, i ^ c) for i in range(devices)])  9.23 us
    dot_general x1, matrix products, run(): jnp.einsum('mnj,nb->jmb', merge_tensor, local_two, precision=high)  7.26 us
    dot_general x1, matrix products, run(): weave = jnp.einsum('ma,jmb->jab', local_one, folded_local, precision=high)  6.57 us
    dot_general x1, local copies, waits for them, and re-layouts, run(): jnp.einsum('mnj,nb->jmb', merge_tensor, local_two, precision=high)  3.12 us
    slice x1, local copies, waits for them, and re-layouts, run(): proj_one = prepared(mode_rows_one, sample_counts[0], branch_one)  1.32 us
  transfers between devices with their start and end apart: 9, of which 5 were waited for; matrix products, arithmetic and copies ran while one was open for 0% of the time, Pallas kernels for 0%

profile of v1, /device:TPU:0, one launch (start us, length us, event | category | flops | bytes accessed | tf_op | source)
XLA Modules:
  0.0 63.1 jit_solution(12466054783647331536)
XLA Ops:
  0.0 0.0 copy-start
  0.0 1.3 %fusion.38 = (s32[1]{0:T(128)}, s32[1]{0:T(128)}) fusion(s32[2]{0:T(128)} %param.7), kind=kLoop, calls=%fused_computation.57 | loop fusion | bytes 16 | tf_op jit(solution)/shard_map/slice | solution.py:88
  1.4 0.6 iota_compare_fusion.1
  1.9 0.1 dynamic-slice
  2.0 0.9 %constant_dynamic-slice_fusion.1 = f32[96,64]{1,0:T(8,128)S(1)} fusion(f32[96,256]{1,0:T(8,128)} %param.9, s32[]{:T(128)S(6)} %select_n.14), kind=kLoop, calls=%fused_computation.54 | loop fusion | bytes 49156 | tf_op jit(solution)/shard_map/dynamic_slice | solution.py:94
  2.9 0.1 copy.40
  2.9 7.3 %fusion.17 = f32[64,96,96]{2,0,1:T(8,128)} fusion(f32[96,96,96]{2,1,0:T(8,128)} %param.10, f32[96,64]{0,1:T(8,128)S(1)} %copy.40, f32[96]{0:T(128)S(1)} %fusion.33, pred[64]{0:T(512)(128)(4,1)S(1)} %dynamic-slice), kind=kOutput, calls=%fused_computation.29 | convolution fusion | flops 679489536 | bytes 5923264 | tf_op jit(solution)/shard_map/mnj,nb->jmb/dot_general | solution.py:95
  10.2 0.0 copy-start.1
  10.2 3.1 %copy.31 = f32[64,96,96]{1,2,0:T(8,128)S(1)} copy(f32[64,96,96]{2,0,1:T(8,128)} %fusion.17) | data formatting | bytes 4718592 | tf_op jit(solution)/shard_map/mnj,nb->jmb/dot_general | solution.py:95
  13.3 0.6 iota_compare_fusion
  14.0 0.1 dynamic-slice.1
  14.1 0.0 copy-done.1
  14.1 0.1 constant_dynamic-slice_fusion
  14.1 0.1 copy.41
  14.2 6.6 %fusion.2 = f32[96,32,64]{0,1,2:T(8,128)S(1)} fusion(f32[64,96,96]{1,2,0:T(8,128)S(1)} %copy.31, f32[96,32]{0,1:T(8,128)S(1)} %copy.41, f32[96]{0:T(128)S(1)} %fusion.35, pred[32]{0:T(512)(128)(4,1)S(1)} %dynamic-slice.1), kind=kOutput, calls=%fused_computation.2 | convolution fusion | flops 226498560 | bytes 3158432 | tf_op jit(solution)/shard_map/ma,jmb->jab/dot_general | solution.py:96
  20.8 0.6 copy.20
  21.4 0.3 copy.21
  21.7 0.1 reduce-precision_convert_fusion
  21.8 0.1 pad_maximum_fusion.weave_ref
  21.9 0.1 pad_add_fusion.where
  22.0 15.5 %shard_map.64 = f32[8,4,96,128]{3,2,1,0:T(8,128)S(1)} custom-call(s32[2]{0:T(128)S(1)} %pad_add_fusion.where, f32[2048,4096]{1,0:T(8,128)} %bitcast.83, bf16[192,2048]{1,0:T(8,128)(2,1)S(1)} %pad_maximum_fusion.weave_ref), custom_call_target="tpu_custom_call" | custom-call | tf_op jit(solution)/shard_map/pallas_call | solution.py:44
  37.5 0.1 slice_bitcast_fusion
  37.6 0.6 collective-permute-start
  38.1 1.9 %collective-permute-done = f32[2,2,2,2,96,128]{5,4,3,2,1,0:T(8,128)S(1)} collective-permute-done((f32[2,2,2,2,96,128]{5,4,3,2,1,0:T(8,128)S(1)}, f32[2,2,2,2,96,128]{5,4,3,2,1,0:T(8,128)S(1)}, u32[]{:S(2)}, u32[]{:S(2)}) %collective-permute-start) | collective-permute-done | bytes 786464 | tf_op jit(solution)/shard_map/ppermute | solution.py:72
  40.0 0.1 fusion.6
  40.2 3.0 %collective-permute-start.1 = (f32[2,96,128]{2,1,0:T(8,128)S(1)}, f32[2,96,128]{2,1,0:T(8,128)S(1)}, u32[]{:S(2)}, u32[]{:S(2)}) collective-permute-start(f32[2,96,128]{2,1,0:T(8,128)S(1)} %get-tuple-element.5), channel_id=1, source_target_pairs={{0,8},{1,9},{2,10},{3,11},{4,12},{5,13},{6,14},{7,15},{8,0},{9,1},... | collective-permute-start | bytes 294920 | tf_op jit(solution)/shard_map/ppermute | solution.py:72
  43.2 1.5 %collective-permute-start.2 = (f32[2,96,128]{2,1,0:T(8,128)S(1)}, f32[2,96,128]{2,1,0:T(8,128)S(1)}, u32[]{:S(2)}, u32[]{:S(2)}) collective-permute-start(f32[2,96,128]{2,1,0:T(8,128)S(1)} %get-tuple-element.9), channel_id=1, source_target_pairs={{0,4},{1,5},{2,6},{3,7},{4,0},{5,1},{6,2},{7,3},{8,12},{9,13},{10,... | collective-permute-start | bytes 294920 | tf_op jit(solution)/shard_map/ppermute | solution.py:72
  44.7 0.0 collective-permute-start.3
  44.7 1.9 %collective-permute-start.4 = (f32[2,96,128]{2,1,0:T(8,128)S(1)}, f32[2,96,128]{2,1,0:T(8,128)S(1)}, u32[]{:S(2)}, u32[]{:S(2)}) collective-permute-start(f32[2,96,128]{2,1,0:T(8,128)S(1)} %get-tuple-element.7), channel_id=1, source_target_pairs={{0,2},{1,3},{2,0},{3,1},{4,6},{5,7},{6,4},{7,5},{8,10},{9,11},{10,... | collective-permute-start | bytes 294920 | tf_op jit(solution)/shard_map/ppermute | solution.py:72
  46.6 1.6 %collective-permute-start.5 = (f32[2,96,128]{2,1,0:T(8,128)S(1)}, f32[2,96,128]{2,1,0:T(8,128)S(1)}, u32[]{:S(2)}, u32[]{:S(2)}) collective-permute-start(f32[2,96,128]{2,1,0:T(8,128)S(1)} %get-tuple-element.6), channel_id=1, source_target_pairs={{0,10},{1,11},{2,8},{3,9},{4,14},{5,15},{6,12},{7,13},{8,2},{9,3},... | collective-permute-start | bytes 294920 | tf_op jit(solution)/shard_map/ppermute | solution.py:72
  48.1 0.0 collective-permute-done.1
  48.2 2.4 %collective-permute-start.6 = (f32[2,96,128]{2,1,0:T(8,128)S(1)}, f32[2,96,128]{2,1,0:T(8,128)S(1)}, u32[]{:S(2)}, u32[]{:S(2)}) collective-permute-start(f32[2,96,128]{2,1,0:T(8,128)S(1)} %get-tuple-element.11), channel_id=1, source_target_pairs={{0,6},{1,7},{2,4},{3,5},{4,2},{5,3},{6,0},{7,1},{8,14},{9,15},{10,... | collective-permute-start | bytes 294920 | tf_op jit(solution)/shard_map/ppermute | solution.py:72
  50.6 0.0 collective-permute-done.2
  50.6 1.5 %collective-permute-start.7 = (f32[2,96,128]{2,1,0:T(8,128)S(1)}, f32[2,96,128]{2,1,0:T(8,128)S(1)}, u32[]{:S(2)}, u32[]{:S(2)}) collective-permute-start(f32[2,96,128]{2,1,0:T(8,128)S(1)} %get-tuple-element.10), channel_id=1, source_target_pairs={{0,14},{1,15},{2,12},{3,13},{4,10},{5,11},{6,8},{7,9},{8,6},{9,7},... | collective-permute-start | bytes 294920 | tf_op jit(solution)/shard_map/ppermute | solution.py:72
  52.1 0.0 collective-permute-done.3
  52.1 0.0 collective-permute-done.4
  52.1 0.2 collective-permute-done.5
  52.3 3.7 %collective-permute-done.6 = f32[2,96,128]{2,1,0:T(8,128)S(1)} collective-permute-done((f32[2,96,128]{2,1,0:T(8,128)S(1)}, f32[2,96,128]{2,1,0:T(8,128)S(1)}, u32[]{:S(2)}, u32[]{:S(2)}) %collective-permute-start.6) | collective-permute-done | bytes 98336 | tf_op jit(solution)/shard_map/ppermute | solution.py:72
  55.9 1.1 %collective-permute-done.7 = f32[2,96,128]{2,1,0:T(8,128)S(1)} collective-permute-done((f32[2,96,128]{2,1,0:T(8,128)S(1)}, f32[2,96,128]{2,1,0:T(8,128)S(1)}, u32[]{:S(2)}, u32[]{:S(2)}) %collective-permute-start.7) | collective-permute-done | bytes 98336 | tf_op jit(solution)/shard_map/ppermute | solution.py:72
  57.1 2.7 %collective-permute-start.8 = (f32[96,128]{1,0:T(8,128)S(1)}, f32[96,128]{1,0:T(8,128)S(1)}, u32[]{:S(2)}, u32[]{:S(2)}) collective-permute-start(f32[96,128]{1,0:T(8,128)S(1)} %slice_bitcast_fusion.10), channel_id=1, source_target_pairs={{0,16},{1,17},{2,18},{3,19},{4,20},{5,21},{6,22},{7,23},{8,24},{9,... | collective-permute-start | bytes 147464 | tf_op jit(solution)/shard_map/ppermute | solution.py:72
  59.7 2.4 %collective-permute-done.8 = f32[96,128]{1,0:T(8,128)S(1)} collective-permute-done((f32[96,128]{1,0:T(8,128)S(1)}, f32[96,128]{1,0:T(8,128)S(1)}, u32[]{:S(2)}, u32[]{:S(2)}) %collective-permute-start.8) | collective-permute-done | bytes 49184 | tf_op jit(solution)/shard_map/ppermute | solution.py:72
  62.1 0.0 copy-done
  62.1 1.0 %fusion.15 = f32[128,256]{1,0:T(8,128)} fusion(f32[96,256]{1,0:T(8,128)S(1)} %copy-done, f32[96,128]{1,0:T(8,128)S(1)} %collective-permute-done.8, f32[2,96,128]{2,1,0:T(8,128)S(1)} %fusion.13), kind=kOutput, calls=%fused_computation.28 | convolution fusion | flops 37761024 | bytes 327680 | tf_op jit(solution)/shard_map/dot_general | solution.py:110
  (5 shorter events, 0.1 us)
Async XLA Ops:
  0.0 62.1 %copy-start = (f32[96,256]{1,0:T(8,128)S(1)}, f32[96,256]{1,0:T(8,128)}, u32[]{:S(2)}) copy-start(f32[96,256]{1,0:T(8,128)} %param.11) | copy-start | bytes 294916
  10.2 3.8 %copy-start.1 = (f32[96,256]{1,0:T(8,128)S(1)}, f32[96,256]{1,0:T(8,128)}, u32[]{:S(2)}) copy-start(f32[96,256]{1,0:T(8,128)} %param.8) | copy-start | bytes 294916
  37.6 2.5 %collective-permute-start = (f32[2,2,2,2,96,128]{5,4,3,2,1,0:T(8,128)S(1)}, f32[2,2,2,2,96,128]{5,4,3,2,1,0:T(8,128)S(1)}, u32[]{:S(2)}, u32[]{:S(2)}) collective-permute-start(f32[2,2,2,2,96,128]{5,4,3,2,1,0:T(8,128)S(1)} %slice_bitcast_fusion), channel_id=1, source_target_pairs={{0,1},{1,0},{2,3},{3,2},{4,5},{5,4},{6,7},{7,6},{8,9},{9,8},{10,11... | collective-permute-start | bytes 2359304 | tf_op jit(solution)/shard_map/ppermute | solution.py:72
  40.2 8.0 %collective-permute-start.1 = (f32[2,96,128]{2,1,0:T(8,128)S(1)}, f32[2,96,128]{2,1,0:T(8,128)S(1)}, u32[]{:S(2)}, u32[]{:S(2)}) collective-permute-start(f32[2,96,128]{2,1,0:T(8,128)S(1)} %get-tuple-element.5), channel_id=1, source_target_pairs={{0,8},{1,9},{2,10},{3,11},{4,12},{5,13},{6,14},{7,15},{8,0},{9,1},... | collective-permute-start | bytes 294920 | tf_op jit(solution)/shard_map/ppermute | solution.py:72
  43.2 7.4 %collective-permute-start.2 = (f32[2,96,128]{2,1,0:T(8,128)S(1)}, f32[2,96,128]{2,1,0:T(8,128)S(1)}, u32[]{:S(2)}, u32[]{:S(2)}) collective-permute-start(f32[2,96,128]{2,1,0:T(8,128)S(1)} %get-tuple-element.9), channel_id=1, source_target_pairs={{0,4},{1,5},{2,6},{3,7},{4,0},{5,1},{6,2},{7,3},{8,12},{9,13},{10,... | collective-permute-start | bytes 294920 | tf_op jit(solution)/shard_map/ppermute | solution.py:72
  44.7 7.4 %collective-permute-start.3 = (f32[2,96,128]{2,1,0:T(8,128)S(1)}, f32[2,96,128]{2,1,0:T(8,128)S(1)}, u32[]{:S(2)}, u32[]{:S(2)}) collective-permute-start(f32[2,96,128]{2,1,0:T(8,128)S(1)} %get-tuple-element.8), channel_id=1, source_target_pairs={{0,12},{1,13},{2,14},{3,15},{4,8},{5,9},{6,10},{7,11},{8,4},{9,5},... | collective-permute-start | bytes 294920 | tf_op jit(solution)/shard_map/ppermute | solution.py:72
  44.7 7.4 %collective-permute-start.4 = (f32[2,96,128]{2,1,0:T(8,128)S(1)}, f32[2,96,128]{2,1,0:T(8,128)S(1)}, u32[]{:S(2)}, u32[]{:S(2)}) collective-permute-start(f32[2,96,128]{2,1,0:T(8,128)S(1)} %get-tuple-element.7), channel_id=1, source_target_pairs={{0,2},{1,3},{2,0},{3,1},{4,6},{5,7},{6,4},{7,5},{8,10},{9,11},{10,... | collective-permute-start | bytes 294920 | tf_op jit(solution)/shard_map/ppermute | solution.py:72
  46.6 5.7 %collective-permute-start.5 = (f32[2,96,128]{2,1,0:T(8,128)S(1)}, f32[2,96,128]{2,1,0:T(8,128)S(1)}, u32[]{:S(2)}, u32[]{:S(2)}) collective-permute-start(f32[2,96,128]{2,1,0:T(8,128)S(1)} %get-tuple-element.6), channel_id=1, source_target_pairs={{0,10},{1,11},{2,8},{3,9},{4,14},{5,15},{6,12},{7,13},{8,2},{9,3},... | collective-permute-start | bytes 294920 | tf_op jit(solution)/shard_map/ppermute | solution.py:72
  48.2 7.8 %collective-permute-start.6 = (f32[2,96,128]{2,1,0:T(8,128)S(1)}, f32[2,96,128]{2,1,0:T(8,128)S(1)}, u32[]{:S(2)}, u32[]{:S(2)}) collective-permute-start(f32[2,96,128]{2,1,0:T(8,128)S(1)} %get-tuple-element.11), channel_id=1, source_target_pairs={{0,6},{1,7},{2,4},{3,5},{4,2},{5,3},{6,0},{7,1},{8,14},{9,15},{10,... | collective-permute-start | bytes 294920 | tf_op jit(solution)/shard_map/ppermute | solution.py:72
  50.6 6.4 %collective-permute-start.7 = (f32[2,96,128]{2,1,0:T(8,128)S(1)}, f32[2,96,128]{2,1,0:T(8,128)S(1)}, u32[]{:S(2)}, u32[]{:S(2)}) collective-permute-start(f32[2,96,128]{2,1,0:T(8,128)S(1)} %get-tuple-element.10), channel_id=1, source_target_pairs={{0,14},{1,15},{2,12},{3,13},{4,10},{5,11},{6,8},{7,9},{8,6},{9,7},... | collective-permute-start | bytes 294920 | tf_op jit(solution)/shard_map/ppermute | solution.py:72
  57.1 5.1 %collective-permute-start.8 = (f32[96,128]{1,0:T(8,128)S(1)}, f32[96,128]{1,0:T(8,128)S(1)}, u32[]{:S(2)}, u32[]{:S(2)}) collective-permute-start(f32[96,128]{1,0:T(8,128)S(1)} %slice_bitcast_fusion.10), channel_id=1, source_target_pairs={{0,16},{1,17},{2,18},{3,19},{4,20},{5,21},{6,22},{7,23},{8,24},{9,... | collective-permute-start | bytes 147464 | tf_op jit(solution)/shard_map/ppermute | solution.py:72

commit v2 on v1

v2 whole, which is shorter than its diff:
```python
import jax
import jax.numpy as jnp
from jax import lax
from jax.experimental import pallas as pl
from jax.experimental.pallas import tpu as pltpu
from jax.sharding import PartitionSpec as P

branch_one = 0.00025
branch_two = 0.0004
AXES = ("pop", "merge")
LANES = 128
SUBLANES = 8


def prepared(rows, count, branch):
    order = jnp.arange(rows.shape[0], dtype=jnp.float32)
    decay = jnp.exp(-branch * order * (order + 1.0) / 2.0)
    keep = jnp.arange(rows.shape[1], dtype=jnp.int32) <= count
    return jnp.where(keep[None, :], rows, jnp.zeros_like(rows)) * decay[:, None]


def split(value):
    high = value.astype(jnp.bfloat16)
    return high, (value - high.astype(jnp.float32)).astype(jnp.bfloat16)


def product(stacked, count, value):
    high, low = split(value)
    two = jnp.dot(stacked, high, preferred_element_type=jnp.float32)
    one = jnp.dot(stacked[:count], low, preferred_element_type=jnp.float32)
    return two[:count] + (two[count:] + one)


def partial_sums(slab, counts, rows_one, rows_two, merge_tensor, local_one, local_two, pops, merges):
    rows, cols = slab.shape
    modes = rows_one.shape[0]
    per = cols // (pops * merges)
    wide = merges * per
    step_one = local_two + SUBLANES
    padded = pl.cdiv(modes, LANES) * LANES

    def body(
        counts_ref, one_ref, two_ref, tensor_ref, slab_ref, out_ref,
        tensor_buf, slab_buf, rows_buf, folded_ref, woven_ref, weave_ref, tensor_sem, slab_sems,
    ):
        pop = lax.axis_index("pop")
        merge = lax.axis_index("merge")
        tensor_copy = pltpu.make_async_copy(tensor_ref, tensor_buf, tensor_sem)
        tensor_copy.start()

        def slab_copy(i):
            at = pl.multiple_of(jnp.bitwise_xor(i, pop) * wide, LANES)
            return pltpu.make_async_copy(
                slab_ref.at[:, pl.ds(at, wide)], slab_buf.at[i], slab_sems.at[i]
            )

        def local(ref, count, branch, begin, size):
            full = jnp.concatenate(
                [ref[...], jnp.zeros((padded - modes, ref.shape[1]), jnp.float32)], axis=0
            )
            rows_buf[: ref.shape[1]] = full.T
            mine = rows_buf[pl.ds(pl.multiple_of(begin, SUBLANES), size)]
            order = lax.broadcasted_iota(jnp.int32, mine.shape, 1).astype(jnp.float32)
            decay = jnp.exp(-branch * order * (order + 1.0) / 2.0)
            entry = lax.broadcasted_iota(jnp.int32, mine.shape, 0) + begin
            mine = jnp.where(entry <= count, mine, 0.0) * decay
            return jnp.concatenate(split(mine[:, :modes]), axis=0)

        proj_two = local(two_ref, counts_ref[1], branch_two, merge * local_two, local_two)
        proj_one = local(one_ref, counts_ref[0], branch_one, pop * local_one, local_one)
        tensor_copy.wait()
        for i in range(pops):
            slab_copy(i).start()

        def fold(m, carry):
            at = pl.multiple_of(m * step_one, SUBLANES)
            folded_ref[pl.ds(at, local_two), :modes] = product(proj_two, local_two, tensor_buf[m])
            return carry

        lax.fori_loop(0, modes, fold, 0, unroll=8)

        def weave(b, carry):
            value = folded_ref[pl.ds(b, modes, stride=step_one), :]
            woven_ref[pl.ds(b, local_one, stride=step_one), :] = product(proj_one, local_one, value)
            return carry

        lax.fori_loop(0, local_two, weave, 0, unroll=8)

        group = LANES // local_two
        for q in range(local_one // group):
            value = jnp.concatenate(
                [woven_ref[pl.ds((q * group + k) * step_one, local_two), :] for k in range(group)],
                axis=0,
            )
            high, low = split(value.T[:modes])
            weave_ref[:modes, q * LANES : (q + 1) * LANES] = high
            weave_ref[modes:, q * LANES : (q + 1) * LANES] = low

        def block(i, carry):
            slab_copy(i).wait()
            value = product(weave_ref[...], modes, slab_buf[i])
            for m in range(merges):
                out_ref[i, jnp.bitwise_xor(merge, m)] = value[:, m * per : (m + 1) * per]
            return carry

        lax.fori_loop(0, pops, block, 0)

    vmem = pl.BlockSpec(memory_space=pltpu.VMEM)
    hbm = pl.BlockSpec(memory_space=pl.ANY)
    return pl.pallas_call(
        body,
        out_shape=jax.ShapeDtypeStruct((pops, merges, modes, per), jnp.float32),
        in_specs=[pl.BlockSpec(memory_space=pltpu.SMEM), vmem, vmem, hbm, hbm],
        out_specs=vmem,
        scratch_shapes=[
            pltpu.VMEM(merge_tensor.shape, jnp.float32),
            pltpu.VMEM((pops, rows, wide), jnp.float32),
            pltpu.VMEM((max(rows_one.shape[1], rows_two.shape[1]), padded), jnp.float32),
            pltpu.VMEM((modes * step_one, padded), jnp.float32),
            pltpu.VMEM((local_one * step_one, padded), jnp.float32),
            pltpu.VMEM((2 * modes, rows), jnp.bfloat16),
            pltpu.SemaphoreType.DMA,
            pltpu.SemaphoreType.DMA((pops,)),
        ],
        compiler_params=pltpu.CompilerParams(vmem_limit_bytes=56 * 1024 * 1024),
    )(counts, rows_one, rows_two, merge_tensor, slab)


def scatter_sum(value, devices):
    bits = [1 << k for k in reversed(range(devices.bit_length() - 1))]
    value = value.reshape((2,) * len(bits) + value.shape[-2:])
    for group in ([bits[-1]], bits[1:-1], [bits[0]]):
        combos = [0]
        for bit in group:
            combos = combos + [c | bit for c in combos]

        def piece(c):
            return value[tuple((1 if c & b else 0) if b in group else slice(None) for b in bits)]

        sent = [
            lax.ppermute(piece(c), AXES, [(i, i ^ c) for i in range(devices)]) for c in combos[1:]
        ]
        total = piece(0)
        for part in sent:
            total = total + part
        value = total
        bits = [b for b in bits if b not in group]
    return value


def on_device(pops, merges):
    devices = pops * merges

    def run(slab, sample_counts, mode_rows_one, mode_rows_two, merge_tensor, ancestral_modes):
        high = lax.Precision.HIGHEST
        modes = mode_rows_one.shape[0]
        local_one, local_two, cols = slab.shape
        flat_slab = slab.reshape(local_one * local_two, cols)
        two_power = devices & (devices - 1) == 0 and pops > 2 and merges > 1
        tiles = local_one % SUBLANES == 0 and local_two % SUBLANES == 0 and LANES % local_two == 0
        if two_power and tiles and cols % (devices * LANES) == 0:
            parts = partial_sums(
                flat_slab, sample_counts, mode_rows_one, mode_rows_two, merge_tensor,
                local_one, local_two, pops, merges,
            )
            summed = scatter_sum(parts, devices)
        else:
            proj_one = prepared(mode_rows_one, sample_counts[0], branch_one)
            proj_two = prepared(mode_rows_two, sample_counts[1], branch_two)
            begin_one = lax.axis_index("pop") * local_one
            begin_two = lax.axis_index("merge") * local_two
            mine_one = lax.dynamic_slice_in_dim(proj_one, begin_one, local_one, 1)
            mine_two = lax.dynamic_slice_in_dim(proj_two, begin_two, local_two, 1)
            folded = jnp.einsum("mnj,nb->jmb", merge_tensor, mine_two, precision=high)
            weave = jnp.einsum("ma,jmb->jab", mine_one, folded, precision=high)
            weave = weave.reshape(modes, local_one * local_two)
            summed = lax.psum_scatter(
                lax.dot_general(weave, flat_slab, (((1,), (0,)), ((), ())), precision=high),
                AXES,
                scatter_dimension=1,
                tiled=True,
            )
        return lax.dot_general(summed, ancestral_modes, (((0,), (0,)), ((), ())), precision=high)

    return run


def solution(mesh):
    in_specs = (P("pop", "merge", None), P(), P(), P(), P(), P())
    out_specs = P(AXES, None)
    run = on_device(mesh.shape["pop"], mesh.shape["merge"])
    return jax.shard_map(run, mesh=mesh, in_specs=in_specs, out_specs=out_specs, check_vma=False)
```

time: 63.5 us -> 46.2 us (0.73)
  matrix products: 14.8 us -> 0.97 us
  local copies, waits for them, and re-layouts: 6.74 us -> 1.38 us
  Pallas kernels: 15.5 us -> 18.3 us
  other arithmetic: 1.62 us -> 0.14 us
  waiting for transfers between devices: 9.23 us -> 10 us
    dot_general x2 -> x0, matrix products: 13.8 us -> none  [the longest x1 7.26 us: run(): jnp.einsum('mnj,nb->jmb', merge_tensor, local_two, precision=high)]
    dot_general x1 -> x0, local copies, waits for them, and re-layouts: 3.12 us -> none  [run(): jnp.einsum('mnj,nb->jmb', merge_tensor, local_two, precision=high)]
    pallas_call x1, Pallas kernels: 15.5 us -> 18.3 us  [partial_sums(): pl.pallas_call(body, out_shape=jax.ShapeDtypeStruct((pops, merges, modes,...]
    slice x1 -> x0, local copies, waits for them, and re-layouts: 1.32 us -> none  [run(): proj_one = prepared(mode_rows_one, sample_counts[0], branch_one)]
    squeeze x3, local copies, waits for them, and re-layouts: 0.12 us -> 1.37 us  [piece(): value[tuple(((1 if c & b else 0) if b in group else slice(None) for b in...]
    le x2 -> x0, other arithmetic: 1.19 us -> none  [prepared(): keep = jnp.arange(rows.shape[1], dtype=jnp.int32) <= count]
    dynamic_slice x4 -> x0, local copies, waits for them, and re-layouts: 1.11 us -> none  [the longest x2 0.95 us: run(): local_two = lax.dynamic_slice_in_dim(proj_two, begin_two, rows_two, 1)]
    ppermute x9, waiting for transfers between devices: 9.23 us -> 10 us  [scatter_sum(): lax.ppermute(piece(c), AXES, [(i, i ^ c) for i in range(devices)])]
  transfers between devices with their start and end apart: 9 -> 9, of which waited for: 5 -> 4; matrix products, arithmetic and copies ran while one was open for 0% -> 0% of each run, Pallas kernels for 0% -> 0%
where the time goes in v2:
time: 46.2 us; the launch traced here: 46 us
  Pallas kernels  18.3 us (40%)
  starting transfers between devices  15.2 us (33%)
  waiting for transfers between devices  10 us (22%)
  local copies, waits for them, and re-layouts  1.38 us (3%)
  matrix products  0.97 us (2%)
    pallas_call x1, Pallas kernels, partial_sums(): pl.pallas_call(body, out_shape=jax.ShapeDtypeStruct((pops, merges, modes,...  18.3 us
    ppermute x9, starting transfers between devices, scatter_sum(): lax.ppermute(piece(c), AXES, [(i, i ^ c) for i in range(devices)])  15.2 us
    ppermute x9, waiting for transfers between devices, scatter_sum(): lax.ppermute(piece(c), AXES, [(i, i ^ c) for i in range(devices)])  10 us
    squeeze x3, local copies, waits for them, and re-layouts, piece(): value[tuple(((1 if c & b else 0) if b in group else slice(None) for b in...  1.37 us
    dot_general x1, matrix products, run(): lax.dot_general(summed, ancestral_modes, (((0,), (0,)), ((), ())), precis...  0.97 us
  transfers between devices with their start and end apart: 9, of which 4 were waited for; matrix products, arithmetic and copies ran while one was open for 0% of the time, Pallas kernels for 0%

profile of v2, /device:TPU:0, one launch (start us, length us, event | category | flops | bytes accessed | tf_op | source)
XLA Modules:
  0.0 46.0 jit_solution(12748212957833286130)
XLA Ops:
  0.0 0.0 copy-start
  0.0 18.3 %shard_map.64 = f32[8,4,96,128]{3,2,1,0:T(8,128)} custom-call(s32[2]{0:T(128)} %counts_ref.1, f32[96,256]{1,0:T(8,128)} %one_ref.1, f32[96,256]{1,0:T(8,128)} %two_ref.1, f32[96,96,96]{2,1,0:T(8,128)} %tensor_ref.1, f32[2048,4096]{1,0:T(8,128)} %bitcast.62), custom_call_target="tpu_custom_call" | custom-call | tf_op jit(solution)/shard_map/pallas_call | solution.py:110
  18.3 0.0 copy-start.1
  18.3 1.3 %slice_bitcast_fusion = f32[2,2,2,2,96,128]{5,4,3,2,1,0:T(8,128)S(1)} fusion(f32[2,2,2,2,2,96,128]{6,5,4,3,2,1,0:T(8,128)} %bitcast.63), kind=kLoop, calls=%fused_computation | loop fusion | bytes 1572864 | tf_op jit(solution)/shard_map/squeeze | solution.py:138
  19.6 0.6 %collective-permute-start = (f32[2,2,2,2,96,128]{5,4,3,2,1,0:T(8,128)S(1)}, f32[2,2,2,2,96,128]{5,4,3,2,1,0:T(8,128)S(1)}, u32[]{:S(2)}, u32[]{:S(2)}) collective-permute-start(f32[2,2,2,2,96,128]{5,4,3,2,1,0:T(8,128)S(1)} %slice_bitcast_fusion), channel_id=1, source_target_pairs={{0,1},{1,0},{2,3},{3,2},{4,5},{5,4},{6,7},{7,6},{8,9},{9,8},{10,11... | collective-permute-start | bytes 2359304 | tf_op jit(solution)/shard_map/ppermute | solution.py:141
  20.2 1.9 %collective-permute-done = f32[2,2,2,2,96,128]{5,4,3,2,1,0:T(8,128)S(1)} collective-permute-done((f32[2,2,2,2,96,128]{5,4,3,2,1,0:T(8,128)S(1)}, f32[2,2,2,2,96,128]{5,4,3,2,1,0:T(8,128)S(1)}, u32[]{:S(2)}, u32[]{:S(2)}) %collective-permute-start) | collective-permute-done | bytes 786464 | tf_op jit(solution)/shard_map/ppermute | solution.py:141
  22.1 0.0 copy-done.1
  22.1 0.1 fusion
  22.2 3.0 %collective-permute-start.1 = (f32[2,96,128]{2,1,0:T(8,128)S(1)}, f32[2,96,128]{2,1,0:T(8,128)S(1)}, u32[]{:S(2)}, u32[]{:S(2)}) collective-permute-start(f32[2,96,128]{2,1,0:T(8,128)S(1)} %get-tuple-element.5), channel_id=1, source_target_pairs={{0,8},{1,9},{2,10},{3,11},{4,12},{5,13},{6,14},{7,15},{8,0},{9,1},... | collective-permute-start | bytes 294920 | tf_op jit(solution)/shard_map/ppermute | solution.py:141
  25.2 1.4 %collective-permute-start.5 = (f32[2,96,128]{2,1,0:T(8,128)S(1)}, f32[2,96,128]{2,1,0:T(8,128)S(1)}, u32[]{:S(2)}, u32[]{:S(2)}) collective-permute-start(f32[2,96,128]{2,1,0:T(8,128)S(1)} %get-tuple-element.6), channel_id=1, source_target_pairs={{0,10},{1,11},{2,8},{3,9},{4,14},{5,15},{6,12},{7,13},{8,2},{9,3},... | collective-permute-start | bytes 294920 | tf_op jit(solution)/shard_map/ppermute | solution.py:141
  26.6 0.2 collective-permute-start.4
  26.8 2.9 %collective-permute-start.3 = (f32[2,96,128]{2,1,0:T(8,128)S(1)}, f32[2,96,128]{2,1,0:T(8,128)S(1)}, u32[]{:S(2)}, u32[]{:S(2)}) collective-permute-start(f32[2,96,128]{2,1,0:T(8,128)S(1)} %get-tuple-element.8), channel_id=1, source_target_pairs={{0,12},{1,13},{2,14},{3,15},{4,8},{5,9},{6,10},{7,11},{8,4},{9,5},... | collective-permute-start | bytes 294920 | tf_op jit(solution)/shard_map/ppermute | solution.py:141
  29.7 0.5 %collective-permute-start.2 = (f32[2,96,128]{2,1,0:T(8,128)S(1)}, f32[2,96,128]{2,1,0:T(8,128)S(1)}, u32[]{:S(2)}, u32[]{:S(2)}) collective-permute-start(f32[2,96,128]{2,1,0:T(8,128)S(1)} %get-tuple-element.9), channel_id=1, source_target_pairs={{0,4},{1,5},{2,6},{3,7},{4,0},{5,1},{6,2},{7,3},{8,12},{9,13},{10,... | collective-permute-start | bytes 294920 | tf_op jit(solution)/shard_map/ppermute | solution.py:141
  30.2 0.0 collective-permute-done.1
  30.2 2.6 %collective-permute-start.7 = (f32[2,96,128]{2,1,0:T(8,128)S(1)}, f32[2,96,128]{2,1,0:T(8,128)S(1)}, u32[]{:S(2)}, u32[]{:S(2)}) collective-permute-start(f32[2,96,128]{2,1,0:T(8,128)S(1)} %get-tuple-element.10), channel_id=1, source_target_pairs={{0,14},{1,15},{2,12},{3,13},{4,10},{5,11},{6,8},{7,9},{8,6},{9,7},... | collective-permute-start | bytes 294920 | tf_op jit(solution)/shard_map/ppermute | solution.py:141
  32.8 0.0 collective-permute-done.5
  32.8 1.4 %collective-permute-start.6 = (f32[2,96,128]{2,1,0:T(8,128)S(1)}, f32[2,96,128]{2,1,0:T(8,128)S(1)}, u32[]{:S(2)}, u32[]{:S(2)}) collective-permute-start(f32[2,96,128]{2,1,0:T(8,128)S(1)} %get-tuple-element.11), channel_id=1, source_target_pairs={{0,6},{1,7},{2,4},{3,5},{4,2},{5,3},{6,0},{7,1},{8,14},{9,15},{10,... | collective-permute-start | bytes 294920 | tf_op jit(solution)/shard_map/ppermute | solution.py:141
  34.2 0.0 collective-permute-done.4
  34.2 0.1 collective-permute-done.3
  34.3 5.1 %collective-permute-done.2 = f32[2,96,128]{2,1,0:T(8,128)S(1)} collective-permute-done((f32[2,96,128]{2,1,0:T(8,128)S(1)}, f32[2,96,128]{2,1,0:T(8,128)S(1)}, u32[]{:S(2)}, u32[]{:S(2)}) %collective-permute-start.2) | collective-permute-done | bytes 98336 | tf_op jit(solution)/shard_map/ppermute | solution.py:141
  39.4 0.0 collective-permute-done.7
  39.4 0.0 collective-permute-done.6
  39.5 2.7 %collective-permute-start.8 = (f32[96,128]{1,0:T(8,128)S(1)}, f32[96,128]{1,0:T(8,128)S(1)}, u32[]{:S(2)}, u32[]{:S(2)}) collective-permute-start(f32[96,128]{1,0:T(8,128)S(1)} %slice_bitcast_fusion.10), channel_id=1, source_target_pairs={{0,16},{1,17},{2,18},{3,19},{4,20},{5,21},{6,22},{7,23},{8,24},{9,... | collective-permute-start | bytes 147464 | tf_op jit(solution)/shard_map/ppermute | solution.py:141
  42.1 2.9 %collective-permute-done.8 = f32[96,128]{1,0:T(8,128)S(1)} collective-permute-done((f32[96,128]{1,0:T(8,128)S(1)}, f32[96,128]{1,0:T(8,128)S(1)}, u32[]{:S(2)}, u32[]{:S(2)}) %collective-permute-start.8) | collective-permute-done | bytes 49184 | tf_op jit(solution)/shard_map/ppermute | solution.py:141
  45.1 0.0 copy-done
  45.1 1.0 %fusion.9 = f32[128,256]{1,0:T(8,128)} fusion(f32[96,256]{1,0:T(8,128)S(1)} %copy-done, f32[96,128]{1,0:T(8,128)S(1)} %collective-permute-done.8, f32[2,96,128]{2,1,0:T(8,128)S(1)} %fusion.7), kind=kOutput, calls=%fused_computation.21 | convolution fusion | flops 37761024 | bytes 327680 | tf_op jit(solution)/shard_map/dot_general | solution.py:183
  (3 shorter events, 0.1 us)
Async XLA Ops:
  0.0 45.1 %copy-start = (f32[96,256]{1,0:T(8,128)S(1)}, f32[96,256]{1,0:T(8,128)}, u32[]{:S(2)}) copy-start(f32[96,256]{1,0:T(8,128)} %param.11) | copy-start | bytes 294916
  18.3 3.8 %copy-start.1 = (f32[8,4,96,128]{3,2,1,0:T(8,128)S(1)}, f32[8,4,96,128]{3,2,1,0:T(8,128)}, u32[]{:S(2)}) copy-start(f32[8,4,96,128]{3,2,1,0:T(8,128)} %shard_map.64) | copy-start | bytes 4718596
  19.6 2.5 %collective-permute-start = (f32[2,2,2,2,96,128]{5,4,3,2,1,0:T(8,128)S(1)}, f32[2,2,2,2,96,128]{5,4,3,2,1,0:T(8,128)S(1)}, u32[]{:S(2)}, u32[]{:S(2)}) collective-permute-start(f32[2,2,2,2,96,128]{5,4,3,2,1,0:T(8,128)S(1)} %slice_bitcast_fusion), channel_id=1, source_target_pairs={{0,1},{1,0},{2,3},{3,2},{4,5},{5,4},{6,7},{7,6},{8,9},{9,8},{10,11... | collective-permute-start | bytes 2359304 | tf_op jit(solution)/shard_map/ppermute | solution.py:141
  22.2 8.0 %collective-permute-start.1 = (f32[2,96,128]{2,1,0:T(8,128)S(1)}, f32[2,96,128]{2,1,0:T(8,128)S(1)}, u32[]{:S(2)}, u32[]{:S(2)}) collective-permute-start(f32[2,96,128]{2,1,0:T(8,128)S(1)} %get-tuple-element.5), channel_id=1, source_target_pairs={{0,8},{1,9},{2,10},{3,11},{4,12},{5,13},{6,14},{7,15},{8,0},{9,1},... | collective-permute-start | bytes 294920 | tf_op jit(solution)/shard_map/ppermute | solution.py:141
  25.2 7.5 %collective-permute-start.5 = (f32[2,96,128]{2,1,0:T(8,128)S(1)}, f32[2,96,128]{2,1,0:T(8,128)S(1)}, u32[]{:S(2)}, u32[]{:S(2)}) collective-permute-start(f32[2,96,128]{2,1,0:T(8,128)S(1)} %get-tuple-element.6), channel_id=1, source_target_pairs={{0,10},{1,11},{2,8},{3,9},{4,14},{5,15},{6,12},{7,13},{8,2},{9,3},... | collective-permute-start | bytes 294920 | tf_op jit(solution)/shard_map/ppermute | solution.py:141
  26.6 7.6 %collective-permute-start.4 = (f32[2,96,128]{2,1,0:T(8,128)S(1)}, f32[2,96,128]{2,1,0:T(8,128)S(1)}, u32[]{:S(2)}, u32[]{:S(2)}) collective-permute-start(f32[2,96,128]{2,1,0:T(8,128)S(1)} %get-tuple-element.7), channel_id=1, source_target_pairs={{0,2},{1,3},{2,0},{3,1},{4,6},{5,7},{6,4},{7,5},{8,10},{9,11},{10,... | collective-permute-start | bytes 294920 | tf_op jit(solution)/shard_map/ppermute | solution.py:141
  26.8 7.5 %collective-permute-start.3 = (f32[2,96,128]{2,1,0:T(8,128)S(1)}, f32[2,96,128]{2,1,0:T(8,128)S(1)}, u32[]{:S(2)}, u32[]{:S(2)}) collective-permute-start(f32[2,96,128]{2,1,0:T(8,128)S(1)} %get-tuple-element.8), channel_id=1, source_target_pairs={{0,12},{1,13},{2,14},{3,15},{4,8},{5,9},{6,10},{7,11},{8,4},{9,5},... | collective-permute-start | bytes 294920 | tf_op jit(solution)/shard_map/ppermute | solution.py:141
  29.7 9.7 %collective-permute-start.2 = (f32[2,96,128]{2,1,0:T(8,128)S(1)}, f32[2,96,128]{2,1,0:T(8,128)S(1)}, u32[]{:S(2)}, u32[]{:S(2)}) collective-permute-start(f32[2,96,128]{2,1,0:T(8,128)S(1)} %get-tuple-element.9), channel_id=1, source_target_pairs={{0,4},{1,5},{2,6},{3,7},{4,0},{5,1},{6,2},{7,3},{8,12},{9,13},{10,... | collective-permute-start | bytes 294920 | tf_op jit(solution)/shard_map/ppermute | solution.py:141
  30.2 9.2 %collective-permute-start.7 = (f32[2,96,128]{2,1,0:T(8,128)S(1)}, f32[2,96,128]{2,1,0:T(8,128)S(1)}, u32[]{:S(2)}, u32[]{:S(2)}) collective-permute-start(f32[2,96,128]{2,1,0:T(8,128)S(1)} %get-tuple-element.10), channel_id=1, source_target_pairs={{0,14},{1,15},{2,12},{3,13},{4,10},{5,11},{6,8},{7,9},{8,6},{9,7},... | collective-permute-start | bytes 294920 | tf_op jit(solution)/shard_map/ppermute | solution.py:141
  32.8 6.6 %collective-permute-start.6 = (f32[2,96,128]{2,1,0:T(8,128)S(1)}, f32[2,96,128]{2,1,0:T(8,128)S(1)}, u32[]{:S(2)}, u32[]{:S(2)}) collective-permute-start(f32[2,96,128]{2,1,0:T(8,128)S(1)} %get-tuple-element.11), channel_id=1, source_target_pairs={{0,6},{1,7},{2,4},{3,5},{4,2},{5,3},{6,0},{7,1},{8,14},{9,15},{10,... | collective-permute-start | bytes 294920 | tf_op jit(solution)/shard_map/ppermute | solution.py:141
  39.5 5.6 %collective-permute-start.8 = (f32[96,128]{1,0:T(8,128)S(1)}, f32[96,128]{1,0:T(8,128)S(1)}, u32[]{:S(2)}, u32[]{:S(2)}) collective-permute-start(f32[96,128]{1,0:T(8,128)S(1)} %slice_bitcast_fusion.10), channel_id=1, source_target_pairs={{0,16},{1,17},{2,18},{3,19},{4,20},{5,21},{6,22},{7,23},{8,24},{9,... | collective-permute-start | bytes 147464 | tf_op jit(solution)/shard_map/ppermute | solution.py:141

commit v3 on v2

--- a/solution.py
+++ b/solution.py
@@ -10,6 +10,8 @@
 AXES = ("pop", "merge")
 LANES = 128
 SUBLANES = 8
+CHUNKS = 3
+VMEM = 56 * 1024 * 1024
 
 
 def prepared(rows, count, branch):
@@ -29,6 +31,12 @@
     two = jnp.dot(stacked, high, preferred_element_type=jnp.float32)
     one = jnp.dot(stacked[:count], low, preferred_element_type=jnp.float32)
     return two[:count] + (two[count:] + one)
+
+
+def store(out_ref, i, merge, value, merges, per):
+    for m in range(merges):
+        r = jnp.bitwise_xor(merge, m)
+        out_ref[r % 2, i, r // 2] = value[:, m * per : (m + 1) * per]
 
 
 def partial_sums(slab, counts, rows_one, rows_two, merge_tensor, local_one, local_two, pops, merges):
@@ -41,18 +49,31 @@
 
     def body(
         counts_ref, one_ref, two_ref, tensor_ref, slab_ref, out_ref,
-        tensor_buf, slab_buf, rows_buf, folded_ref, woven_ref, weave_ref, tensor_sem, slab_sems,
+        one_buf, two_buf, tensor_buf, slab_buf, rows_buf, folded_ref, woven_ref, weave_ref,
+        rows_sems, tensor_sems, slab_sems,
     ):
         pop = lax.axis_index("pop")
         merge = lax.axis_index("merge")
-        tensor_copy = pltpu.make_async_copy(tensor_ref, tensor_buf, tensor_sem)
-        tensor_copy.start()
+        chunk = modes // CHUNKS
+
+        def tensor_copy(k):
+            at = pl.ds(k * chunk, chunk)
+            return pltpu.make_async_copy(tensor_ref.at[at], tensor_buf.at[at], tensor_sems.at[k])
+
+        two_copy = pltpu.make_async_copy(two_ref, two_buf, rows_sems.at[0])
+        one_copy = pltpu.make_async_copy(one_ref, one_buf, rows_sems.at[1])
+        two_copy.start()
+        one_copy.start()
+        for k in range(CHUNKS):
+            tensor_copy(k).start()
 
         def slab_copy(i):
             at = pl.multiple_of(jnp.bitwise_xor(i, pop) * wide, LANES)
             return pltpu.make_async_copy(
                 slab_ref.at[:, pl.ds(at, wide)], slab_buf.at[i], slab_sems.at[i]
             )
+
+        slab_copy(0).start()
 
         def local(ref, count, branch, begin, size):
             full = jnp.concatenate(
@@ -66,25 +87,28 @@
             mine = jnp.where(entry <= count, mine, 0.0) * decay
             return jnp.concatenate(split(mine[:, :modes]), axis=0)
 
-        proj_two = local(two_ref, counts_ref[1], branch_two, merge * local_two, local_two)
-        proj_one = local(one_ref, counts_ref[0], branch_one, pop * local_one, local_one)
-        tensor_copy.wait()
-        for i in range(pops):
-            slab_copy(i).start()
+        two_copy.wait()
+        proj_two = local(two_buf, counts_ref[1], branch_two, merge * local_two, local_two)
+        one_copy.wait()
+        proj_one = local(one_buf, counts_ref[0], branch_one, pop * local_one, local_one)
 
         def fold(m, carry):
             at = pl.multiple_of(m * step_one, SUBLANES)
             folded_ref[pl.ds(at, local_two), :modes] = product(proj_two, local_two, tensor_buf[m])
             return carry
 
-        lax.fori_loop(0, modes, fold, 0, unroll=8)
+        for k in range(CHUNKS):
+            tensor_copy(k).wait()
+            for i in range(1 + k * (pops - 1) // CHUNKS, 1 + (k + 1) * (pops - 1) // CHUNKS):
+                slab_copy(i).start()
+            lax.fori_loop(k * chunk, (k + 1) * chunk, fold, 0, unroll=32)
 
         def weave(b, carry):
             value = folded_ref[pl.ds(b, modes, stride=step_one), :]
             woven_ref[pl.ds(b, local_one, stride=step_one), :] = product(proj_one, local_one, value)
             return carry
 
-        lax.fori_loop(0, local_two, weave, 0, unroll=8)
+        lax.fori_loop(0, local_two, weave, 0, unroll=32)
 
         group = LANES // local_two
         for q in range(local_one // group):
@@ -96,56 +120,51 @@
             weave_ref[:modes, q * LANES : (q + 1) * LANES] = high
             weave_ref[modes:, q * LANES : (q + 1) * LANES] = low
 
-        def block(i, carry):
+        for i in range(pops):
             slab_copy(i).wait()
-            value = product(weave_ref[...], modes, slab_buf[i])
-            for m in range(merges):
-                out_ref[i, jnp.bitwise_xor(merge, m)] = value[:, m * per : (m + 1) * per]
-            return carry
-
-        lax.fori_loop(0, pops, block, 0)
+            store(out_ref, i, merge, product(weave_ref[...], modes, slab_buf[i]), merges, per)
 
     vmem = pl.BlockSpec(memory_space=pltpu.VMEM)
-    hbm = pl.BlockSpec(memory_space=pl.ANY)
+    hbm = pl.BlockSpec(memory_space=pltpu.HBM)
     return pl.pallas_call(
         body,
-        out_shape=jax.ShapeDtypeStruct((pops, merges, modes, per), jnp.float32),
-        in_specs=[pl.BlockSpec(memory_space=pltpu.SMEM), vmem, vmem, hbm, hbm],
+        out_shape=pltpu.VMEM((2, pops, merges // 2, modes, per), jnp.float32),
+        in_specs=[pl.BlockSpec(memory_space=pltpu.SMEM), hbm, hbm, hbm, hbm],
         out_specs=vmem,
         scratch_shapes=[
+            pltpu.VMEM(rows_one.shape, jnp.float32),
+            pltpu.VMEM(rows_two.shape, jnp.float32),
             pltpu.VMEM(merge_tensor.shape, jnp.float32),
             pltpu.VMEM((pops, rows, wide), jnp.float32),
             pltpu.VMEM((max(rows_one.shape[1], rows_two.shape[1]), padded), jnp.float32),
             pltpu.VMEM((modes * step_one, padded), jnp.float32),
             pltpu.VMEM((local_one * step_one, padded), jnp.float32),
             pltpu.VMEM((2 * modes, rows), jnp.bfloat16),
-            pltpu.SemaphoreType.DMA,
+            pltpu.SemaphoreType.DMA((2,)),
+            pltpu.SemaphoreType.DMA((CHUNKS,)),
             pltpu.SemaphoreType.DMA((pops,)),
         ],
-        compiler_params=pltpu.CompilerParams(vmem_limit_bytes=56 * 1024 * 1024),
+        compiler_params=pltpu.CompilerParams(vmem_limit_bytes=VMEM),
     )(counts, rows_one, rows_two, merge_tensor, slab)
 
 
-def scatter_sum(value, devices):
-    bits = [1 << k for k in reversed(range(devices.bit_length() - 1))]
-    value = value.reshape((2,) * len(bits) + value.shape[-2:])
-    for group in ([bits[-1]], bits[1:-1], [bits[0]]):
-        combos = [0]
-        for bit in group:
-            combos = combos + [c | bit for c in combos]
-
-        def piece(c):
-            return value[tuple((1 if c & b else 0) if b in group else slice(None) for b in bits)]
-
-        sent = [
-            lax.ppermute(piece(c), AXES, [(i, i ^ c) for i in range(devices)]) for c in combos[1:]
-        ]
-        total = piece(0)
-        for part in sent:
-            total = total + part
-        value = total
-        bits = [b for b in bits if b not in group]
-    return value
+def direct_sum(value, bits, group, devices):
+    combos = [0]
+    for bit in group:
+        combos = combos + [c | bit for c in combos]
+
+    def piece(c):
+        return value[tuple((1 if c & b else 0) if b in group else slice(None) for b in bits)]
+
+    sent = [to(piece(c), c, devices) for c in combos[1:]]
+    total = piece(0)
+    for part in sent:
+        total = total + part
+    return total
+
+
+def to(value, bit, devices):
+    return lax.ppermute(value, AXES, [(i, i ^ bit) for i in range(devices)])
 
 
 def on_device(pops, merges):
@@ -156,14 +175,18 @@
         modes = mode_rows_one.shape[0]
         local_one, local_two, cols = slab.shape
         flat_slab = slab.reshape(local_one * local_two, cols)
-        two_power = devices & (devices - 1) == 0 and pops > 2 and merges > 1
-        tiles = local_one % SUBLANES == 0 and local_two % SUBLANES == 0 and LANES % local_two == 0
+        two_power = devices & (devices - 1) == 0 and pops > 4 and merges > 1
+        tiles = local_one % SUBLANES == 0 and local_two % SUBLANES == 0 and LANES % local_two == 0 and modes % CHUNKS == 0
         if two_power and tiles and cols % (devices * LANES) == 0:
             parts = partial_sums(
                 flat_slab, sample_counts, mode_rows_one, mode_rows_two, merge_tensor,
                 local_one, local_two, pops, merges,
             )
-            summed = scatter_sum(parts, devices)
+            summed = parts[0] + to(parts[1], 1, devices)
+            bits = [1 << k for k in reversed(range(1, devices.bit_length() - 1))]
+            summed = summed.reshape((2,) * len(bits) + summed.shape[-2:])
+            summed = direct_sum(summed, bits, bits[1:], devices)
+            summed = direct_sum(summed, bits[:1], bits[:1], devices)
         else:
             proj_one = prepared(mode_rows_one, sample_counts[0], branch_one)
             proj_two = prepared(mode_rows_two, sample_counts[1], branch_two)

time: 46.2 us -> 41.4 us (0.90)
  Pallas kernels: 18.3 us -> 14.8 us
  local copies, waits for them, and re-layouts: 1.38 us -> 0.11 us
    pallas_call x1, Pallas kernels: 18.3 us -> 14.8 us  [partial_sums(): pl.pallas_call(body, out_shape=pltpu.VMEM((2, pops, merges // 2, modes, p...]
    squeeze x3 -> x2, local copies, waits for them, and re-layouts: 1.37 us -> 0.05 us  [piece(): value[tuple(((1 if c & b else 0) if b in group else slice(None) for b in...]
where the time goes in v3:
time: 41.4 us; the launch traced here: 41.3 us
  starting transfers between devices  15.2 us (37%)
  Pallas kernels  14.8 us (36%)
  waiting for transfers between devices  10 us (24%)
  matrix products  0.97 us (2%)
    ppermute x9, starting transfers between devices, to(): return lax.ppermute(value, AXES, [(i, i ^ bit) for i in range(devices)])  15.2 us
    pallas_call x1, Pallas kernels, partial_sums(): pl.pallas_call(body, out_shape=pltpu.VMEM((2, pops, merges // 2, modes, p...  14.8 us
    ppermute x9, waiting for transfers between devices, to(): return lax.ppermute(value, AXES, [(i, i ^ bit) for i in range(devices)])  10 us
    dot_general x1, matrix products, run(): lax.dot_general(summed, ancestral_modes, (((0,), (0,)), ((), ())), precis...  0.97 us
  transfers between devices with their start and end apart: 9, of which 4 were waited for; matrix products, arithmetic and copies ran while one was open for 0% of the time, Pallas kernels for 0%

profile of v3, /device:TPU:0, one launch (start us, length us, event | category | flops | bytes accessed | tf_op | source)
XLA Modules:
  0.0 41.3 jit_solution(1113464171764185156)
XLA Ops:
  0.0 0.0 copy-start
  0.0 14.8 %shard_map.64 = f32[2,8,2,96,128]{4,3,2,1,0:T(8,128)S(1)} custom-call(s32[2]{0:T(128)} %counts_ref.1, f32[96,256]{1,0:T(8,128)} %one_ref.1, f32[96,256]{1,0:T(8,128)} %two_ref.1, f32[96,96,96]{2,1,0:T(8,128)} %tensor_ref.1, f32[2048,4096]{1,0:T(8,128)} %bitcast.60), custom_call_target="tpu_custom_call" | custom-call | tf_op jit(solution)/shard_map/pallas_call | solution.py:129
  14.8 0.1 slice_bitcast_fusion
  14.9 0.6 %collective-permute-start = (f32[8,2,96,128]{3,2,1,0:T(8,128)S(1)}, f32[8,2,96,128]{3,2,1,0:T(8,128)S(1)}, u32[]{:S(2)}, u32[]{:S(2)}) collective-permute-start(f32[8,2,96,128]{3,2,1,0:T(8,128)S(1)} %slice_bitcast_fusion), channel_id=1, source_target_pairs={{0,1},{1,0},{2,3},{3,2},{4,5},{5,4},{6,7},{7,6},{8,9},{9,8},{10,11... | collective-permute-start | bytes 2359304 | tf_op jit(solution)/shard_map/ppermute | solution.py:167
  15.4 1.9 %collective-permute-done = f32[8,2,96,128]{3,2,1,0:T(8,128)S(1)} collective-permute-done((f32[8,2,96,128]{3,2,1,0:T(8,128)S(1)}, f32[8,2,96,128]{3,2,1,0:T(8,128)S(1)}, u32[]{:S(2)}, u32[]{:S(2)}) %collective-permute-start) | collective-permute-done | bytes 786464 | tf_op jit(solution)/shard_map/ppermute | solution.py:167
  17.3 0.1 fusion
  17.5 3.0 %collective-permute-start.1 = (f32[2,96,128]{2,1,0:T(8,128)S(1)}, f32[2,96,128]{2,1,0:T(8,128)S(1)}, u32[]{:S(2)}, u32[]{:S(2)}) collective-permute-start(f32[2,96,128]{2,1,0:T(8,128)S(1)} %get-tuple-element.5), channel_id=1, source_target_pairs={{0,8},{1,9},{2,10},{3,11},{4,12},{5,13},{6,14},{7,15},{8,0},{9,1},... | collective-permute-start | bytes 294920 | tf_op jit(solution)/shard_map/ppermute | solution.py:167
  20.5 1.4 %collective-permute-start.5 = (f32[2,96,128]{2,1,0:T(8,128)S(1)}, f32[2,96,128]{2,1,0:T(8,128)S(1)}, u32[]{:S(2)}, u32[]{:S(2)}) collective-permute-start(f32[2,96,128]{2,1,0:T(8,128)S(1)} %get-tuple-element.6), channel_id=1, source_target_pairs={{0,10},{1,11},{2,8},{3,9},{4,14},{5,15},{6,12},{7,13},{8,2},{9,3},... | collective-permute-start | bytes 294920 | tf_op jit(solution)/shard_map/ppermute | solution.py:167
  21.9 0.2 collective-permute-start.4
  22.0 2.9 %collective-permute-start.3 = (f32[2,96,128]{2,1,0:T(8,128)S(1)}, f32[2,96,128]{2,1,0:T(8,128)S(1)}, u32[]{:S(2)}, u32[]{:S(2)}) collective-permute-start(f32[2,96,128]{2,1,0:T(8,128)S(1)} %get-tuple-element.8), channel_id=1, source_target_pairs={{0,12},{1,13},{2,14},{3,15},{4,8},{5,9},{6,10},{7,11},{8,4},{9,5},... | collective-permute-start | bytes 294920 | tf_op jit(solution)/shard_map/ppermute | solution.py:167
  24.9 0.5 %collective-permute-start.2 = (f32[2,96,128]{2,1,0:T(8,128)S(1)}, f32[2,96,128]{2,1,0:T(8,128)S(1)}, u32[]{:S(2)}, u32[]{:S(2)}) collective-permute-start(f32[2,96,128]{2,1,0:T(8,128)S(1)} %get-tuple-element.9), channel_id=1, source_target_pairs={{0,4},{1,5},{2,6},{3,7},{4,0},{5,1},{6,2},{7,3},{8,12},{9,13},{10,... | collective-permute-start | bytes 294920 | tf_op jit(solution)/shard_map/ppermute | solution.py:167
  25.4 0.0 collective-permute-done.1
  25.4 2.6 %collective-permute-start.7 = (f32[2,96,128]{2,1,0:T(8,128)S(1)}, f32[2,96,128]{2,1,0:T(8,128)S(1)}, u32[]{:S(2)}, u32[]{:S(2)}) collective-permute-start(f32[2,96,128]{2,1,0:T(8,128)S(1)} %get-tuple-element.10), channel_id=1, source_target_pairs={{0,14},{1,15},{2,12},{3,13},{4,10},{5,11},{6,8},{7,9},{8,6},{9,7},... | collective-permute-start | bytes 294920 | tf_op jit(solution)/shard_map/ppermute | solution.py:167
  28.0 0.0 collective-permute-done.5
  28.0 1.5 %collective-permute-start.6 = (f32[2,96,128]{2,1,0:T(8,128)S(1)}, f32[2,96,128]{2,1,0:T(8,128)S(1)}, u32[]{:S(2)}, u32[]{:S(2)}) collective-permute-start(f32[2,96,128]{2,1,0:T(8,128)S(1)} %get-tuple-element.11), channel_id=1, source_target_pairs={{0,6},{1,7},{2,4},{3,5},{4,2},{5,3},{6,0},{7,1},{8,14},{9,15},{10,... | collective-permute-start | bytes 294920 | tf_op jit(solution)/shard_map/ppermute | solution.py:167
  29.5 0.0 collective-permute-done.4
  29.5 0.1 collective-permute-done.3
  29.6 5.1 %collective-permute-done.2 = f32[2,96,128]{2,1,0:T(8,128)S(1)} collective-permute-done((f32[2,96,128]{2,1,0:T(8,128)S(1)}, f32[2,96,128]{2,1,0:T(8,128)S(1)}, u32[]{:S(2)}, u32[]{:S(2)}) %collective-permute-start.2) | collective-permute-done | bytes 98336 | tf_op jit(solution)/shard_map/ppermute | solution.py:167
  34.6 0.0 collective-permute-done.7
  34.7 0.0 collective-permute-done.6
  34.7 2.7 %collective-permute-start.8 = (f32[96,128]{1,0:T(8,128)S(1)}, f32[96,128]{1,0:T(8,128)S(1)}, u32[]{:S(2)}, u32[]{:S(2)}) collective-permute-start(f32[96,128]{1,0:T(8,128)S(1)} %slice_bitcast_fusion.10), channel_id=1, source_target_pairs={{0,16},{1,17},{2,18},{3,19},{4,20},{5,21},{6,22},{7,23},{8,24},{9,... | collective-permute-start | bytes 147464 | tf_op jit(solution)/shard_map/ppermute | solution.py:167
  37.4 2.9 %collective-permute-done.8 = f32[96,128]{1,0:T(8,128)S(1)} collective-permute-done((f32[96,128]{1,0:T(8,128)S(1)}, f32[96,128]{1,0:T(8,128)S(1)}, u32[]{:S(2)}, u32[]{:S(2)}) %collective-permute-start.8) | collective-permute-done | bytes 49184 | tf_op jit(solution)/shard_map/ppermute | solution.py:167
  40.3 0.0 copy-done
  40.3 1.0 %fusion.9 = f32[128,256]{1,0:T(8,128)} fusion(f32[96,256]{1,0:T(8,128)S(1)} %copy-done, f32[96,128]{1,0:T(8,128)S(1)} %collective-permute-done.8, f32[2,96,128]{2,1,0:T(8,128)S(1)} %fusion.7), kind=kOutput, calls=%fused_computation.21 | convolution fusion | flops 37761024 | bytes 327680 | tf_op jit(solution)/shard_map/dot_general | solution.py:206
  (3 shorter events, 0.1 us)
Async XLA Ops:
  0.0 40.3 %copy-start = (f32[96,256]{1,0:T(8,128)S(1)}, f32[96,256]{1,0:T(8,128)}, u32[]{:S(2)}) copy-start(f32[96,256]{1,0:T(8,128)} %param.11) | copy-start | bytes 294916
  14.9 2.5 %collective-permute-start = (f32[8,2,96,128]{3,2,1,0:T(8,128)S(1)}, f32[8,2,96,128]{3,2,1,0:T(8,128)S(1)}, u32[]{:S(2)}, u32[]{:S(2)}) collective-permute-start(f32[8,2,96,128]{3,2,1,0:T(8,128)S(1)} %slice_bitcast_fusion), channel_id=1, source_target_pairs={{0,1},{1,0},{2,3},{3,2},{4,5},{5,4},{6,7},{7,6},{8,9},{9,8},{10,11... | collective-permute-start | bytes 2359304 | tf_op jit(solution)/shard_map/ppermute | solution.py:167
  17.5 8.0 %collective-permute-start.1 = (f32[2,96,128]{2,1,0:T(8,128)S(1)}, f32[2,96,128]{2,1,0:T(8,128)S(1)}, u32[]{:S(2)}, u32[]{:S(2)}) collective-permute-start(f32[2,96,128]{2,1,0:T(8,128)S(1)} %get-tuple-element.5), channel_id=1, source_target_pairs={{0,8},{1,9},{2,10},{3,11},{4,12},{5,13},{6,14},{7,15},{8,0},{9,1},... | collective-permute-start | bytes 294920 | tf_op jit(solution)/shard_map/ppermute | solution.py:167
  20.5 7.5 %collective-permute-start.5 = (f32[2,96,128]{2,1,0:T(8,128)S(1)}, f32[2,96,128]{2,1,0:T(8,128)S(1)}, u32[]{:S(2)}, u32[]{:S(2)}) collective-permute-start(f32[2,96,128]{2,1,0:T(8,128)S(1)} %get-tuple-element.6), channel_id=1, source_target_pairs={{0,10},{1,11},{2,8},{3,9},{4,14},{5,15},{6,12},{7,13},{8,2},{9,3},... | collective-permute-start | bytes 294920 | tf_op jit(solution)/shard_map/ppermute | solution.py:167
  21.9 7.6 %collective-permute-start.4 = (f32[2,96,128]{2,1,0:T(8,128)S(1)}, f32[2,96,128]{2,1,0:T(8,128)S(1)}, u32[]{:S(2)}, u32[]{:S(2)}) collective-permute-start(f32[2,96,128]{2,1,0:T(8,128)S(1)} %get-tuple-element.7), channel_id=1, source_target_pairs={{0,2},{1,3},{2,0},{3,1},{4,6},{5,7},{6,4},{7,5},{8,10},{9,11},{10,... | collective-permute-start | bytes 294920 | tf_op jit(solution)/shard_map/ppermute | solution.py:167
  22.0 7.5 %collective-permute-start.3 = (f32[2,96,128]{2,1,0:T(8,128)S(1)}, f32[2,96,128]{2,1,0:T(8,128)S(1)}, u32[]{:S(2)}, u32[]{:S(2)}) collective-permute-start(f32[2,96,128]{2,1,0:T(8,128)S(1)} %get-tuple-element.8), channel_id=1, source_target_pairs={{0,12},{1,13},{2,14},{3,15},{4,8},{5,9},{6,10},{7,11},{8,4},{9,5},... | collective-permute-start | bytes 294920 | tf_op jit(solution)/shard_map/ppermute | solution.py:167
  24.9 9.7 %collective-permute-start.2 = (f32[2,96,128]{2,1,0:T(8,128)S(1)}, f32[2,96,128]{2,1,0:T(8,128)S(1)}, u32[]{:S(2)}, u32[]{:S(2)}) collective-permute-start(f32[2,96,128]{2,1,0:T(8,128)S(1)} %get-tuple-element.9), channel_id=1, source_target_pairs={{0,4},{1,5},{2,6},{3,7},{4,0},{5,1},{6,2},{7,3},{8,12},{9,13},{10,... | collective-permute-start | bytes 294920 | tf_op jit(solution)/shard_map/ppermute | solution.py:167
  25.4 9.2 %collective-permute-start.7 = (f32[2,96,128]{2,1,0:T(8,128)S(1)}, f32[2,96,128]{2,1,0:T(8,128)S(1)}, u32[]{:S(2)}, u32[]{:S(2)}) collective-permute-start(f32[2,96,128]{2,1,0:T(8,128)S(1)} %get-tuple-element.10), channel_id=1, source_target_pairs={{0,14},{1,15},{2,12},{3,13},{4,10},{5,11},{6,8},{7,9},{8,6},{9,7},... | collective-permute-start | bytes 294920 | tf_op jit(solution)/shard_map/ppermute | solution.py:167
  28.0 6.6 %collective-permute-start.6 = (f32[2,96,128]{2,1,0:T(8,128)S(1)}, f32[2,96,128]{2,1,0:T(8,128)S(1)}, u32[]{:S(2)}, u32[]{:S(2)}) collective-permute-start(f32[2,96,128]{2,1,0:T(8,128)S(1)} %get-tuple-element.11), channel_id=1, source_target_pairs={{0,6},{1,7},{2,4},{3,5},{4,2},{5,3},{6,0},{7,1},{8,14},{9,15},{10,... | collective-permute-start | bytes 294920 | tf_op jit(solution)/shard_map/ppermute | solution.py:167
  34.7 5.6 %collective-permute-start.8 = (f32[96,128]{1,0:T(8,128)S(1)}, f32[96,128]{1,0:T(8,128)S(1)}, u32[]{:S(2)}, u32[]{:S(2)}) collective-permute-start(f32[96,128]{1,0:T(8,128)S(1)} %slice_bitcast_fusion.10), channel_id=1, source_target_pairs={{0,16},{1,17},{2,18},{3,19},{4,20},{5,21},{6,22},{7,23},{8,24},{9,... | collective-permute-start | bytes 147464 | tf_op jit(solution)/shard_map/ppermute | solution.py:167

commit v4 on v3

--- a/solution.py
+++ b/solution.py
@@ -5,12 +5,14 @@
 from jax.experimental.pallas import tpu as pltpu
 from jax.sharding import PartitionSpec as P
 
+
 branch_one = 0.00025
 branch_two = 0.0004
 AXES = ("pop", "merge")
 LANES = 128
 SUBLANES = 8
 CHUNKS = 3
+AHEAD = 5
 VMEM = 56 * 1024 * 1024
 
 
@@ -99,7 +101,7 @@
 
         for k in range(CHUNKS):
             tensor_copy(k).wait()
-            for i in range(1 + k * (pops - 1) // CHUNKS, 1 + (k + 1) * (pops - 1) // CHUNKS):
+            for i in range(1 + k * (AHEAD - 1) // CHUNKS, 1 + (k + 1) * (AHEAD - 1) // CHUNKS):
                 slab_copy(i).start()
             lax.fori_loop(k * chunk, (k + 1) * chunk, fold, 0, unroll=32)
 
@@ -108,7 +110,7 @@
             woven_ref[pl.ds(b, local_one, stride=step_one), :] = product(proj_one, local_one, value)
             return carry
 
-        lax.fori_loop(0, local_two, weave, 0, unroll=32)
+        lax.fori_loop(0, local_two, weave, 0, unroll=64)
 
         group = LANES // local_two
         for q in range(local_one // group):
@@ -122,6 +124,8 @@
 
         for i in range(pops):
             slab_copy(i).wait()
+            if i + AHEAD < pops:
+                slab_copy(i + AHEAD).start()
             store(out_ref, i, merge, product(weave_ref[...], modes, slab_buf[i]), merges, per)
 
     vmem = pl.BlockSpec(memory_space=pltpu.VMEM)
@@ -156,7 +160,9 @@
     def piece(c):
         return value[tuple((1 if c & b else 0) if b in group else slice(None) for b in bits)]
 
-    sent = [to(piece(c), c, devices) for c in combos[1:]]
+    sent = []
+    for c in combos[1:]:
+        sent.append(to(piece(c), c, devices))
     total = piece(0)
     for part in sent:
         total = total + part
@@ -177,7 +183,7 @@
         flat_slab = slab.reshape(local_one * local_two, cols)
         two_power = devices & (devices - 1) == 0 and pops > 4 and merges > 1
         tiles = local_one % SUBLANES == 0 and local_two % SUBLANES == 0 and LANES % local_two == 0 and modes % CHUNKS == 0
-        if two_power and tiles and cols % (devices * LANES) == 0:
+        if two_power and tiles and pops > AHEAD and cols % (devices * LANES) == 0:
             parts = partial_sums(
                 flat_slab, sample_counts, mode_rows_one, mode_rows_two, merge_tensor,
                 local_one, local_two, pops, merges,

time: 41.4 us -> 41.3 us (level)
  no operation moved by 1% of the time
where the time goes in v4:
time: 41.3 us; the launch traced here: 41.2 us
  starting transfers between devices  15.2 us (37%)
  Pallas kernels  14.7 us (36%)
  waiting for transfers between devices  10 us (24%)
  matrix products  0.97 us (2%)
    ppermute x9, starting transfers between devices, to(): return lax.ppermute(value, AXES, [(i, i ^ bit) for i in range(devices)])  15.2 us
    pallas_call x1, Pallas kernels, partial_sums(): pl.pallas_call(body, out_shape=pltpu.VMEM((2, pops, merges // 2, modes, p...  14.7 us
    ppermute x9, waiting for transfers between devices, to(): return lax.ppermute(value, AXES, [(i, i ^ bit) for i in range(devices)])  10 us
    dot_general x1, matrix products, run(): lax.dot_general(summed, ancestral_modes, (((0,), (0,)), ((), ())), precis...  0.97 us
  transfers between devices with their start and end apart: 9, of which 4 were waited for; matrix products, arithmetic and copies ran while one was open for 0% of the time, Pallas kernels for 0%

profile of v4, /device:TPU:0, one launch (start us, length us, event | category | flops | bytes accessed | tf_op | source)
XLA Modules:
  0.0 41.2 jit_solution(13023826305768282365)
XLA Ops:
  0.0 0.0 copy-start
  0.0 14.7 %shard_map.64 = f32[2,8,2,96,128]{4,3,2,1,0:T(8,128)S(1)} custom-call(s32[2]{0:T(128)} %counts_ref.1, f32[96,256]{1,0:T(8,128)} %one_ref.1, f32[96,256]{1,0:T(8,128)} %two_ref.1, f32[96,96,96]{2,1,0:T(8,128)} %tensor_ref.1, f32[2048,4096]{1,0:T(8,128)} %bitcast.60), custom_call_target="tpu_custom_call" | custom-call | tf_op jit(solution)/shard_map/pallas_call | solution.py:133
  14.7 0.1 slice_bitcast_fusion
  14.8 0.6 %collective-permute-start = (f32[8,2,96,128]{3,2,1,0:T(8,128)S(1)}, f32[8,2,96,128]{3,2,1,0:T(8,128)S(1)}, u32[]{:S(2)}, u32[]{:S(2)}) collective-permute-start(f32[8,2,96,128]{3,2,1,0:T(8,128)S(1)} %slice_bitcast_fusion), channel_id=1, source_target_pairs={{0,1},{1,0},{2,3},{3,2},{4,5},{5,4},{6,7},{7,6},{8,9},{9,8},{10,11... | collective-permute-start | bytes 2359304 | tf_op jit(solution)/shard_map/ppermute | solution.py:173
  15.3 1.9 %collective-permute-done = f32[8,2,96,128]{3,2,1,0:T(8,128)S(1)} collective-permute-done((f32[8,2,96,128]{3,2,1,0:T(8,128)S(1)}, f32[8,2,96,128]{3,2,1,0:T(8,128)S(1)}, u32[]{:S(2)}, u32[]{:S(2)}) %collective-permute-start) | collective-permute-done | bytes 786464 | tf_op jit(solution)/shard_map/ppermute | solution.py:173
  17.2 0.1 fusion
  17.4 3.0 %collective-permute-start.1 = (f32[2,96,128]{2,1,0:T(8,128)S(1)}, f32[2,96,128]{2,1,0:T(8,128)S(1)}, u32[]{:S(2)}, u32[]{:S(2)}) collective-permute-start(f32[2,96,128]{2,1,0:T(8,128)S(1)} %get-tuple-element.5), channel_id=1, source_target_pairs={{0,8},{1,9},{2,10},{3,11},{4,12},{5,13},{6,14},{7,15},{8,0},{9,1},... | collective-permute-start | bytes 294920 | tf_op jit(solution)/shard_map/ppermute | solution.py:173
  20.4 1.4 %collective-permute-start.5 = (f32[2,96,128]{2,1,0:T(8,128)S(1)}, f32[2,96,128]{2,1,0:T(8,128)S(1)}, u32[]{:S(2)}, u32[]{:S(2)}) collective-permute-start(f32[2,96,128]{2,1,0:T(8,128)S(1)} %get-tuple-element.6), channel_id=1, source_target_pairs={{0,10},{1,11},{2,8},{3,9},{4,14},{5,15},{6,12},{7,13},{8,2},{9,3},... | collective-permute-start | bytes 294920 | tf_op jit(solution)/shard_map/ppermute | solution.py:173
  21.7 0.2 collective-permute-start.4
  21.9 2.9 %collective-permute-start.3 = (f32[2,96,128]{2,1,0:T(8,128)S(1)}, f32[2,96,128]{2,1,0:T(8,128)S(1)}, u32[]{:S(2)}, u32[]{:S(2)}) collective-permute-start(f32[2,96,128]{2,1,0:T(8,128)S(1)} %get-tuple-element.8), channel_id=1, source_target_pairs={{0,12},{1,13},{2,14},{3,15},{4,8},{5,9},{6,10},{7,11},{8,4},{9,5},... | collective-permute-start | bytes 294920 | tf_op jit(solution)/shard_map/ppermute | solution.py:173
  24.8 0.5 %collective-permute-start.2 = (f32[2,96,128]{2,1,0:T(8,128)S(1)}, f32[2,96,128]{2,1,0:T(8,128)S(1)}, u32[]{:S(2)}, u32[]{:S(2)}) collective-permute-start(f32[2,96,128]{2,1,0:T(8,128)S(1)} %get-tuple-element.9), channel_id=1, source_target_pairs={{0,4},{1,5},{2,6},{3,7},{4,0},{5,1},{6,2},{7,3},{8,12},{9,13},{10,... | collective-permute-start | bytes 294920 | tf_op jit(solution)/shard_map/ppermute | solution.py:173
  25.3 0.0 collective-permute-done.1
  25.3 2.6 %collective-permute-start.7 = (f32[2,96,128]{2,1,0:T(8,128)S(1)}, f32[2,96,128]{2,1,0:T(8,128)S(1)}, u32[]{:S(2)}, u32[]{:S(2)}) collective-permute-start(f32[2,96,128]{2,1,0:T(8,128)S(1)} %get-tuple-element.10), channel_id=1, source_target_pairs={{0,14},{1,15},{2,12},{3,13},{4,10},{5,11},{6,8},{7,9},{8,6},{9,7},... | collective-permute-start | bytes 294920 | tf_op jit(solution)/shard_map/ppermute | solution.py:173
  27.9 0.0 collective-permute-done.5
  27.9 1.4 %collective-permute-start.6 = (f32[2,96,128]{2,1,0:T(8,128)S(1)}, f32[2,96,128]{2,1,0:T(8,128)S(1)}, u32[]{:S(2)}, u32[]{:S(2)}) collective-permute-start(f32[2,96,128]{2,1,0:T(8,128)S(1)} %get-tuple-element.11), channel_id=1, source_target_pairs={{0,6},{1,7},{2,4},{3,5},{4,2},{5,3},{6,0},{7,1},{8,14},{9,15},{10,... | collective-permute-start | bytes 294920 | tf_op jit(solution)/shard_map/ppermute | solution.py:173
  29.4 0.0 collective-permute-done.4
  29.4 0.1 collective-permute-done.3
  29.5 5.1 %collective-permute-done.2 = f32[2,96,128]{2,1,0:T(8,128)S(1)} collective-permute-done((f32[2,96,128]{2,1,0:T(8,128)S(1)}, f32[2,96,128]{2,1,0:T(8,128)S(1)}, u32[]{:S(2)}, u32[]{:S(2)}) %collective-permute-start.2) | collective-permute-done | bytes 98336 | tf_op jit(solution)/shard_map/ppermute | solution.py:173
  34.5 0.0 collective-permute-done.7
  34.5 0.0 collective-permute-done.6
  34.6 2.7 %collective-permute-start.8 = (f32[96,128]{1,0:T(8,128)S(1)}, f32[96,128]{1,0:T(8,128)S(1)}, u32[]{:S(2)}, u32[]{:S(2)}) collective-permute-start(f32[96,128]{1,0:T(8,128)S(1)} %slice_bitcast_fusion.10), channel_id=1, source_target_pairs={{0,16},{1,17},{2,18},{3,19},{4,20},{5,21},{6,22},{7,23},{8,24},{9,... | collective-permute-start | bytes 147464 | tf_op jit(solution)/shard_map/ppermute | solution.py:173
  37.3 2.9 %collective-permute-done.8 = f32[96,128]{1,0:T(8,128)S(1)} collective-permute-done((f32[96,128]{1,0:T(8,128)S(1)}, f32[96,128]{1,0:T(8,128)S(1)}, u32[]{:S(2)}, u32[]{:S(2)}) %collective-permute-start.8) | collective-permute-done | bytes 49184 | tf_op jit(solution)/shard_map/ppermute | solution.py:173
  40.2 0.0 copy-done
  40.2 1.0 %fusion.9 = f32[128,256]{1,0:T(8,128)} fusion(f32[96,256]{1,0:T(8,128)S(1)} %copy-done, f32[96,128]{1,0:T(8,128)S(1)} %collective-permute-done.8, f32[2,96,128]{2,1,0:T(8,128)S(1)} %fusion.7), kind=kOutput, calls=%fused_computation.21 | convolution fusion | flops 37761024 | bytes 327680 | tf_op jit(solution)/shard_map/dot_general | solution.py:212
  (3 shorter events, 0.1 us)
Async XLA Ops:
  0.0 40.2 %copy-start = (f32[96,256]{1,0:T(8,128)S(1)}, f32[96,256]{1,0:T(8,128)}, u32[]{:S(2)}) copy-start(f32[96,256]{1,0:T(8,128)} %param.11) | copy-start | bytes 294916
  14.8 2.5 %collective-permute-start = (f32[8,2,96,128]{3,2,1,0:T(8,128)S(1)}, f32[8,2,96,128]{3,2,1,0:T(8,128)S(1)}, u32[]{:S(2)}, u32[]{:S(2)}) collective-permute-start(f32[8,2,96,128]{3,2,1,0:T(8,128)S(1)} %slice_bitcast_fusion), channel_id=1, source_target_pairs={{0,1},{1,0},{2,3},{3,2},{4,5},{5,4},{6,7},{7,6},{8,9},{9,8},{10,11... | collective-permute-start | bytes 2359304 | tf_op jit(solution)/shard_map/ppermute | solution.py:173
  17.4 8.0 %collective-permute-start.1 = (f32[2,96,128]{2,1,0:T(8,128)S(1)}, f32[2,96,128]{2,1,0:T(8,128)S(1)}, u32[]{:S(2)}, u32[]{:S(2)}) collective-permute-start(f32[2,96,128]{2,1,0:T(8,128)S(1)} %get-tuple-element.5), channel_id=1, source_target_pairs={{0,8},{1,9},{2,10},{3,11},{4,12},{5,13},{6,14},{7,15},{8,0},{9,1},... | collective-permute-start | bytes 294920 | tf_op jit(solution)/shard_map/ppermute | solution.py:173
  20.4 7.6 %collective-permute-start.5 = (f32[2,96,128]{2,1,0:T(8,128)S(1)}, f32[2,96,128]{2,1,0:T(8,128)S(1)}, u32[]{:S(2)}, u32[]{:S(2)}) collective-permute-start(f32[2,96,128]{2,1,0:T(8,128)S(1)} %get-tuple-element.6), channel_id=1, source_target_pairs={{0,10},{1,11},{2,8},{3,9},{4,14},{5,15},{6,12},{7,13},{8,2},{9,3},... | collective-permute-start | bytes 294920 | tf_op jit(solution)/shard_map/ppermute | solution.py:173
  21.7 7.6 %collective-permute-start.4 = (f32[2,96,128]{2,1,0:T(8,128)S(1)}, f32[2,96,128]{2,1,0:T(8,128)S(1)}, u32[]{:S(2)}, u32[]{:S(2)}) collective-permute-start(f32[2,96,128]{2,1,0:T(8,128)S(1)} %get-tuple-element.7), channel_id=1, source_target_pairs={{0,2},{1,3},{2,0},{3,1},{4,6},{5,7},{6,4},{7,5},{8,10},{9,11},{10,... | collective-permute-start | bytes 294920 | tf_op jit(solution)/shard_map/ppermute | solution.py:173
  21.9 7.5 %collective-permute-start.3 = (f32[2,96,128]{2,1,0:T(8,128)S(1)}, f32[2,96,128]{2,1,0:T(8,128)S(1)}, u32[]{:S(2)}, u32[]{:S(2)}) collective-permute-start(f32[2,96,128]{2,1,0:T(8,128)S(1)} %get-tuple-element.8), channel_id=1, source_target_pairs={{0,12},{1,13},{2,14},{3,15},{4,8},{5,9},{6,10},{7,11},{8,4},{9,5},... | collective-permute-start | bytes 294920 | tf_op jit(solution)/shard_map/ppermute | solution.py:173
  24.8 9.7 %collective-permute-start.2 = (f32[2,96,128]{2,1,0:T(8,128)S(1)}, f32[2,96,128]{2,1,0:T(8,128)S(1)}, u32[]{:S(2)}, u32[]{:S(2)}) collective-permute-start(f32[2,96,128]{2,1,0:T(8,128)S(1)} %get-tuple-element.9), channel_id=1, source_target_pairs={{0,4},{1,5},{2,6},{3,7},{4,0},{5,1},{6,2},{7,3},{8,12},{9,13},{10,... | collective-permute-start | bytes 294920 | tf_op jit(solution)/shard_map/ppermute | solution.py:173
  25.3 9.2 %collective-permute-start.7 = (f32[2,96,128]{2,1,0:T(8,128)S(1)}, f32[2,96,128]{2,1,0:T(8,128)S(1)}, u32[]{:S(2)}, u32[]{:S(2)}) collective-permute-start(f32[2,96,128]{2,1,0:T(8,128)S(1)} %get-tuple-element.10), channel_id=1, source_target_pairs={{0,14},{1,15},{2,12},{3,13},{4,10},{5,11},{6,8},{7,9},{8,6},{9,7},... | collective-permute-start | bytes 294920 | tf_op jit(solution)/shard_map/ppermute | solution.py:173
  27.9 6.6 %collective-permute-start.6 = (f32[2,96,128]{2,1,0:T(8,128)S(1)}, f32[2,96,128]{2,1,0:T(8,128)S(1)}, u32[]{:S(2)}, u32[]{:S(2)}) collective-permute-start(f32[2,96,128]{2,1,0:T(8,128)S(1)} %get-tuple-element.11), channel_id=1, source_target_pairs={{0,6},{1,7},{2,4},{3,5},{4,2},{5,3},{6,0},{7,1},{8,14},{9,15},{10,... | collective-permute-start | bytes 294920 | tf_op jit(solution)/shard_map/ppermute | solution.py:173
  34.6 5.6 %collective-permute-start.8 = (f32[96,128]{1,0:T(8,128)S(1)}, f32[96,128]{1,0:T(8,128)S(1)}, u32[]{:S(2)}, u32[]{:S(2)}) collective-permute-start(f32[96,128]{1,0:T(8,128)S(1)} %slice_bitcast_fusion.10), channel_id=1, source_target_pairs={{0,16},{1,17},{2,18},{3,19},{4,20},{5,21},{6,22},{7,23},{8,24},{9,... | collective-permute-start | bytes 147464 | tf_op jit(solution)/shard_map/ppermute | solution.py:173
